TPU v7x, 1024 devices: a whole 4x4x32 slice. The times are simulated.
1024 devices in a mesh: row: 32 (over x, y, core), th: 4 (over z_hi), ph: 8 (over z_lo).
Axes of the slice: x: 4, y: 4, z: 32 (z_hi: 4, z_lo: 8; z = z_hi * 8 + z_lo), core: 2. Of those that a mesh axis runs over, the one named last changes fastest.
Arguments:
- cells: float32 [8, 128, 64, 1024], P(None, 'row', 'th', 'ph'), may hold values from -2 to 3, as said below
- faces: float32 [3, 128, 64, 1024], P(None, 'row', 'th', 'ph'), may hold values from -3 to 3
Outputs:
- state: float32 [8, 128, 64, 1024], P(None, 'row', 'th', 'ph')
- faces_new: float32 [3, 128, 64, 1024], P(None, 'row', 'th', 'ph')
Inputs may be any that keep to these rules, and one draw needn't show every extreme that they name: `cells`: fields 0 and 4 (density, pressure) lie between 0.2 and 3; fields 1 to 3 between -0.5 and 0.5; fields 5 to 7 between -2 and 2.
All inputs are finite; a program needn't handle non-finite values.
Results may differ from a plain program's by a relative error of at most 0.0003.
Values sent between devices are 32-bit elements; how exact they have to be, the bound alone decides.
A program may use at most 32 MiB of HBM per device.

v0:
```python
import jax
import jax.numpy as jnp
from jax import lax
from jax.sharding import PartitionSpec as P

adiabatic = 5.0 / 3.0
step_size = 0.05


def padded_2(cells, sides, width):
    for axis, dim in sides:
        count = lax.axis_size(axis)
        head = lax.slice_in_dim(cells, 0, width, axis=dim)
        tail = lax.slice_in_dim(cells, cells.shape[dim] - width, cells.shape[dim], axis=dim)
        cells = jnp.concatenate(
            [
                lax.ppermute(tail, axis, [(i, (i + 1) % count) for i in range(count)]),
                cells,
                lax.ppermute(head, axis, [((i + 1) % count, i) for i in range(count)]),
            ],
            axis=dim,
        )
    return cells


def conserved_flux(padded):
    density = padded[0]
    velocity = padded[1:4]
    pressure = padded[4]
    magnetic = padded[5:8]
    kinetic = 0.5 * density * jnp.sum(velocity * velocity, axis=0)
    magnetic_sq = jnp.sum(magnetic * magnetic, axis=0)
    energy = pressure / (adiabatic - 1.0) + kinetic + 0.5 * magnetic_sq
    total_press = pressure + 0.5 * magnetic_sq
    alignment = jnp.sum(velocity * magnetic, axis=0)
    fast_speed = jnp.sqrt((adiabatic * pressure + magnetic_sq) / density)
    conserved = jnp.stack(
        [density, density * velocity[0], density * velocity[1], density * velocity[2], energy]
    )
    fluxes = []
    speeds = []
    for direction in range(3):
        moving = velocity[direction]
        normal_field = magnetic[direction]
        entries = [density * moving]
        for component in range(3):
            moment = density * velocity[component] * moving - magnetic[component] * normal_field
            if component == direction:
                moment = moment + total_press
            entries.append(moment)
        entries.append((energy + total_press) * moving - normal_field * alignment)
        fluxes.append(jnp.stack(entries))
        speeds.append(jnp.abs(moving) + fast_speed)
    return (conserved, fluxes, speeds)


def hydro_change(padded):
    conserved, fluxes, speeds = conserved_flux(padded)
    change = jnp.zeros_like(conserved[:, 1:-1, 1:-1, 1:-1])
    for direction in range(3):
        keeper = [slice(None), slice(1, -1), slice(1, -1), slice(1, -1)]
        keeper[direction + 1] = slice(None)
        lower_cut = [slice(None)] * 4
        upper_cut = [slice(None)] * 4
        lower_cut[direction + 1] = slice(0, -1)
        upper_cut[direction + 1] = slice(1, None)
        state_cut = conserved[tuple(keeper)]
        flux_cut = fluxes[direction][tuple(keeper)]
        speed_cut = speeds[direction][tuple(keeper[1:])]
        wave_speed = jnp.maximum(speed_cut[tuple(lower_cut[1:])], speed_cut[tuple(upper_cut[1:])])
        face_flux = 0.5 * (
            flux_cut[tuple(lower_cut)] + flux_cut[tuple(upper_cut)]
        ) - 0.5 * wave_speed * (state_cut[tuple(upper_cut)] - state_cut[tuple(lower_cut)])
        change = change + face_flux[tuple(upper_cut)] - face_flux[tuple(lower_cut)]
    return conserved[:, 1:-1, 1:-1, 1:-1] - step_size * change


def edge_fields(padded):
    velocity = padded[1:4]
    magnetic = padded[5:8]
    emf_first = -(velocity[1] * magnetic[2] - velocity[2] * magnetic[1])
    emf_second = -(velocity[2] * magnetic[0] - velocity[0] * magnetic[2])
    emf_third = -(velocity[0] * magnetic[1] - velocity[1] * magnetic[0])
    inner = emf_first[1:-1]
    edge_one = 0.25 * (
        inner[:, :-1, :-1] + inner[:, 1:, :-1] + inner[:, :-1, 1:] + inner[:, 1:, 1:]
    )
    inner = emf_second[:, 1:-1, :]
    edge_two = 0.25 * (
        inner[:-1, :, :-1] + inner[1:, :, :-1] + inner[:-1, :, 1:] + inner[1:, :, 1:]
    )
    inner = emf_third[:, :, 1:-1]
    edge_three = 0.25 * (inner[:-1, :-1] + inner[1:, :-1] + inner[:-1, 1:] + inner[1:, 1:])
    return (edge_one, edge_two, edge_three)


def face_advance(first, second, third, edge_one, edge_two, edge_three):
    new_first = first - step_size * (
        edge_three[:, 1:] - edge_three[:, :-1] - (edge_two[:, :, 1:] - edge_two[:, :, :-1])
    )
    new_second = second - step_size * (
        edge_one[:, :, 1:] - edge_one[:, :, :-1] - (edge_three[1:] - edge_three[:-1])
    )
    new_third = third - step_size * (
        edge_two[1:] - edge_two[:-1] - (edge_one[:, 1:] - edge_one[:, :-1])
    )
    return (new_first, new_second, new_third)


def fix_radial(padded, at_bottom, at_top):
    lowest = jnp.where(at_bottom, padded[:, 1:2], padded[:, :1])
    highest = jnp.where(at_top, padded[:, -2:-1], padded[:, -1:])
    return jnp.concatenate([lowest, padded[:, 1:-1], highest], axis=1)


def fix_polar(padded, at_north, at_south):
    field_ids = jnp.arange(padded.shape[0])
    flipper = (
        jnp.where((field_ids == 2) | (field_ids == 7), -1.0, 1.0)
        .astype(jnp.float32)
        .reshape(-1, 1, 1, 1)
    )
    lowest = jnp.where(at_north, padded[:, :, 1:2] * flipper, padded[:, :, :1])
    highest = jnp.where(at_south, padded[:, :, -2:-1] * flipper, padded[:, :, -1:])
    return jnp.concatenate([lowest, padded[:, :, 1:-1], highest], axis=2)


def on_device(cells, faces):
    row_place = lax.axis_index("row")
    polar_place = lax.axis_index("th")
    at_bottom = row_place == 0
    at_top = row_place == lax.axis_size("row") - 1
    at_north = polar_place == 0
    at_south = polar_place == lax.axis_size("th") - 1
    source = jnp.concatenate([cells, faces], axis=0)
    padded = padded_2(source, (("row", 1), ("th", 2), ("ph", 3)), 1)
    padded = fix_radial(padded, at_bottom, at_top)
    padded = fix_polar(padded, at_north, at_south)
    cell_part = padded[:8]
    conserved_new = hydro_change(cell_part)
    edge_one, edge_two, edge_three = edge_fields(cell_part)
    radial_cells = faces.shape[1]
    polar_cells = faces.shape[2]
    first_ext = jnp.concatenate([faces[0], padded[8, -1:, 1:-1, 1:-1]], axis=0)
    second_ext = jnp.concatenate([faces[1], padded[9, 1:-1, -1:, 1:-1]], axis=1)
    third_ext = jnp.concatenate([faces[2], padded[10, 1:-1, 1:-1, -1:]], axis=2)
    new_first, new_second, new_third = face_advance(
        first_ext, second_ext, third_ext, edge_one, edge_two, edge_three
    )
    upper_first = jnp.concatenate(
        [new_first[1:-1], jnp.where(at_top, new_first[-2:-1], new_first[-1:])], axis=0
    )
    upper_second = jnp.concatenate(
        [new_second[:, 1:-1], jnp.where(at_south, 0.0, new_second[:, -1:])], axis=1
    )
    upper_third = new_third[:, :, 1:]
    new_first = new_first[:radial_cells]
    new_second = new_second[:, :polar_cells]
    new_third = new_third[:, :, :-1]
    centred = 0.5 * jnp.stack(
        [new_first + upper_first, new_second + upper_second, new_third + upper_third]
    )
    state = jnp.concatenate([conserved_new, centred], axis=0)
    return (state, jnp.stack([new_first, new_second, new_third]))


def solution(mesh):
    return jax.shard_map(
        on_device,
        mesh=mesh,
        in_specs=(P(None, "row", "th", "ph"), P(None, "row", "th", "ph")),
        out_specs=(P(None, "row", "th", "ph"), P(None, "row", "th", "ph")),
        check_vma=False,
    )
```

profile of v0, /device:TPU:6, one launch (start us, length us, event | category | flops | bytes accessed | tf_op | source)
XLA Modules:
  0.0 79.4 jit_solution(10637666989561143003)
XLA Ops:
  0.6 1.0 %constant_dynamic-update-slice_fusion.1 = f32[11,4,16,128]{3,2,1,0:T(8,128)S(1)} fusion(f32[8,4,16,128]{3,2,1,0:T(8,128)} %param.2), kind=kLoop, calls=%fused_computation.104 | loop fusion | bytes 524288
  1.6 0.9 %constant_dynamic-update-slice_fusion = f32[11,4,16,128]{3,2,1,0:T(8,128)S(1)} fusion(f32[11,4,16,128]{3,2,1,0:T(8,128)S(1)} %constant_dynamic-update-slice_fusion.1, f32[3,4,16,128]{3,2,1,0:T(8,128)} %param.3), kind=kLoop, calls=%fused_computation.103 | loop fusion | bytes 196608 | tf_op jit(solution)/shard_map/concatenate | solution.py:135
  2.6 1.9 %collective-permute-start = (f32[11,1,16,128]{3,2,1,0:T(8,128)S(1)}, f32[11,1,16,128]{3,2,1,0:T(8,128)S(1)}, u32[]{:S(2)}, u32[]{:S(2)}) collective-permute-start(f32[11,1,16,128]{3,2,1,0:T(8,128)S(1)} %get-tuple-element.44), channel_id=1, source_target_pairs={{0,32},{32,64},{64,96},{96,128},{128,160},{160,192},{192,224},{224... | collective-permute-start | bytes 270344 | tf_op jit(solution)/shard_map/ppermute | solution.py:17
  4.5 5.8 %collective-permute-start.1 = (f32[11,1,16,128]{3,2,1,0:T(8,128)S(1)}, f32[11,1,16,128]{3,2,1,0:T(8,128)S(1)}, u32[]{:S(2)}, u32[]{:S(2)}) collective-permute-start(f32[11,1,16,128]{3,2,1,0:T(8,128)S(1)} %get-tuple-element.45), channel_id=1, source_target_pairs={{32,0},{64,32},{96,64},{128,96},{160,128},{192,160},{224,192},{256... | collective-permute-start | bytes 270344 | tf_op jit(solution)/shard_map/ppermute | solution.py:19
  10.3 0.3 collective-permute-done
  10.5 1.8 %collective-permute-done.1 = f32[11,1,16,128]{3,2,1,0:T(8,128)S(1)} collective-permute-done((f32[11,1,16,128]{3,2,1,0:T(8,128)S(1)}, f32[11,1,16,128]{3,2,1,0:T(8,128)S(1)}, u32[]{:S(2)}, u32[]{:S(2)}) %collective-permute-start.1) | collective-permute-done | bytes 90144 | tf_op jit(solution)/shard_map/ppermute | solution.py:19
  12.4 15.7 %collective-permute-start.2 = (f32[11,6,1,128]{3,2,1,0:T(1,128)S(1)}, f32[11,6,1,128]{3,2,1,0:T(1,128)S(1)}, u32[]{:S(2)}, u32[]{:S(2)}) collective-permute-start(f32[11,6,1,128]{3,2,1,0:T(1,128)S(1)} %get-tuple-element.33), channel_id=1, source_target_pairs={{0,8},{8,16},{16,24},{24,0},{1,9},{9,17},{17,25},{25,1},{2,10},{10... | collective-permute-start | bytes 101384 | tf_op jit(solution)/shard_map/ppermute | solution.py:17
  28.2 9.2 %collective-permute-start.3 = (f32[11,6,1,128]{3,2,1,0:T(1,128)S(1)}, f32[11,6,1,128]{3,2,1,0:T(1,128)S(1)}, u32[]{:S(2)}, u32[]{:S(2)}) collective-permute-start(f32[11,6,1,128]{3,2,1,0:T(1,128)S(1)} %get-tuple-element.34), channel_id=1, source_target_pairs={{8,0},{16,8},{24,16},{0,24},{9,1},{17,9},{25,17},{1,25},{10,2},{18... | collective-permute-start | bytes 101384 | tf_op jit(solution)/shard_map/ppermute | solution.py:19
  37.4 9.8 %collective-permute-done.3 = f32[11,6,1,128]{3,2,1,0:T(1,128)S(1)} collective-permute-done((f32[11,6,1,128]{3,2,1,0:T(1,128)S(1)}, f32[11,6,1,128]{3,2,1,0:T(1,128)S(1)}, u32[]{:S(2)}, u32[]{:S(2)}) %collective-permute-start.3) | collective-permute-done | bytes 33824 | tf_op jit(solution)/shard_map/ppermute | solution.py:19
  47.4 0.3 fusion.38
  47.6 0.5 copy.33
  48.1 0.5 copy.34
  48.6 8.6 %collective-permute-start.5 = (f32[11,6,18,1]{2,3,1,0:T(1,128)S(1)}, f32[11,6,18,1]{2,3,1,0:T(1,128)S(1)}, u32[]{:S(2)}, u32[]{:S(2)}) collective-permute-start(f32[11,6,18,1]{2,3,1,0:T(1,128)S(1)} %copy.34), channel_id=1, source_target_pairs={{1,0},{2,1},{3,2},{4,3},{5,4},{6,5},{7,6},{0,7},{9,8},{10,9},{11,1... | collective-permute-start | bytes 14264 | tf_op jit(solution)/shard_map/ppermute | solution.py:19
  57.2 1.9 %collective-permute-start.4 = (f32[11,6,18,1]{2,3,1,0:T(1,128)S(1)}, f32[11,6,18,1]{2,3,1,0:T(1,128)S(1)}, u32[]{:S(2)}, u32[]{:S(2)}) collective-permute-start(f32[11,6,18,1]{2,3,1,0:T(1,128)S(1)} %copy.33), channel_id=1, source_target_pairs={{0,1},{1,2},{2,3},{3,4},{4,5},{5,6},{6,7},{7,0},{8,9},{9,10},{10,1... | collective-permute-start | bytes 14264 | tf_op jit(solution)/shard_map/ppermute | solution.py:17
  59.2 10.4 %collective-permute-done.4 = f32[11,6,18,1]{2,3,1,0:T(1,128)S(1)} collective-permute-done((f32[11,6,18,1]{2,3,1,0:T(1,128)S(1)}, f32[11,6,18,1]{2,3,1,0:T(1,128)S(1)}, u32[]{:S(2)}, u32[]{:S(2)}) %collective-permute-start.4) | collective-permute-done | bytes 4784 | tf_op jit(solution)/shard_map/ppermute | solution.py:17
  69.7 0.5 copy.28
  70.2 0.5 copy.29
  70.7 1.0 %pad_maximum_fusion = f32[11,6,18,130]{3,2,1,0:T(8,128)S(1)} fusion(f32[11,6,18,1]{3,2,1,0:T(8,128)S(1)} %copy.29, f32[11,6,1,128]{3,2,1,0:T(1,128)S(1)} %collective-permute-done.3, f32[11,1,16,128]{3,2,1,0:T(8,128)S(1)} %collective-permute-done.1, f32[11,4,16,128]{3,2,1,0:T(8,128)S(1)} %constant_dynamic-update-slice_fusion, ...), kind=kLoop, calls=%fused_computation | loop fusion | flops 926640 | bytes 1235520 | tf_op jit(solution)/shard_map/concatenate | solution.py:15
  71.8 0.4 maximum_select_fusion
  72.3 0.4 maximum_select_fusion.1
  72.6 0.2 pad_maximum_fusion.1
  72.8 0.2 slice.459
  73.0 0.2 broadcast_select_fusion.1
  73.3 0.3 pad_maximum_fusion.2
  74.9 0.4 copy-done
  76.3 0.7 copy-done.1
  77.0 0.3 fusion.7
  77.3 0.3 fusion.4
  77.6 0.2 fusion.1
  77.9 0.2 fusion.10
  78.1 0.7 pad_maximum_fusion.4
  78.8 0.6 pad_maximum_fusion.13
  (54 shorter events, 2.6 us)
Async XLA Ops:
  0.6 36.7 %copy-start.2 = (f32[3,4,16,128]{3,2,1,0:T(8,128)S(1)}, f32[3,4,16,128]{3,2,1,0:T(8,128)}, u32[]{:S(2)}) copy-start(f32[3,4,16,128]{3,2,1,0:T(8,128)} %param.3) | copy-start | bytes 294916
  2.6 8.0 %collective-permute-start = (f32[11,1,16,128]{3,2,1,0:T(8,128)S(1)}, f32[11,1,16,128]{3,2,1,0:T(8,128)S(1)}, u32[]{:S(2)}, u32[]{:S(2)}) collective-permute-start(f32[11,1,16,128]{3,2,1,0:T(8,128)S(1)} %get-tuple-element.44), channel_id=1, source_target_pairs={{0,32},{32,64},{64,96},{96,128},{128,160},{160,192},{192,224},{224... | collective-permute-start | bytes 270344 | tf_op jit(solution)/shard_map/ppermute | solution.py:17
  4.5 7.9 %collective-permute-start.1 = (f32[11,1,16,128]{3,2,1,0:T(8,128)S(1)}, f32[11,1,16,128]{3,2,1,0:T(8,128)S(1)}, u32[]{:S(2)}, u32[]{:S(2)}) collective-permute-start(f32[11,1,16,128]{3,2,1,0:T(8,128)S(1)} %get-tuple-element.45), channel_id=1, source_target_pairs={{32,0},{64,32},{96,64},{128,96},{160,128},{192,160},{224,192},{256... | collective-permute-start | bytes 270344 | tf_op jit(solution)/shard_map/ppermute | solution.py:19
  12.4 25.0 %collective-permute-start.2 = (f32[11,6,1,128]{3,2,1,0:T(1,128)S(1)}, f32[11,6,1,128]{3,2,1,0:T(1,128)S(1)}, u32[]{:S(2)}, u32[]{:S(2)}) collective-permute-start(f32[11,6,1,128]{3,2,1,0:T(1,128)S(1)} %get-tuple-element.33), channel_id=1, source_target_pairs={{0,8},{8,16},{16,24},{24,0},{1,9},{9,17},{17,25},{25,1},{2,10},{10... | collective-permute-start | bytes 101384 | tf_op jit(solution)/shard_map/ppermute | solution.py:17
  28.2 19.1 %collective-permute-start.3 = (f32[11,6,1,128]{3,2,1,0:T(1,128)S(1)}, f32[11,6,1,128]{3,2,1,0:T(1,128)S(1)}, u32[]{:S(2)}, u32[]{:S(2)}) collective-permute-start(f32[11,6,1,128]{3,2,1,0:T(1,128)S(1)} %get-tuple-element.34), channel_id=1, source_target_pairs={{8,0},{16,8},{24,16},{0,24},{9,1},{17,9},{25,17},{1,25},{10,2},{18... | collective-permute-start | bytes 101384 | tf_op jit(solution)/shard_map/ppermute | solution.py:19
  48.6 21.6 %collective-permute-start.5 = (f32[11,6,18,1]{2,3,1,0:T(1,128)S(1)}, f32[11,6,18,1]{2,3,1,0:T(1,128)S(1)}, u32[]{:S(2)}, u32[]{:S(2)}) collective-permute-start(f32[11,6,18,1]{2,3,1,0:T(1,128)S(1)} %copy.34), channel_id=1, source_target_pairs={{1,0},{2,1},{3,2},{4,3},{5,4},{6,5},{7,6},{0,7},{9,8},{10,9},{11,1... | collective-permute-start | bytes 14264 | tf_op jit(solution)/shard_map/ppermute | solution.py:19
  57.2 12.4 %collective-permute-start.4 = (f32[11,6,18,1]{2,3,1,0:T(1,128)S(1)}, f32[11,6,18,1]{2,3,1,0:T(1,128)S(1)}, u32[]{:S(2)}, u32[]{:S(2)}) collective-permute-start(f32[11,6,18,1]{2,3,1,0:T(1,128)S(1)} %copy.33), channel_id=1, source_target_pairs={{0,1},{1,2},{2,3},{3,4},{4,5},{5,6},{6,7},{7,0},{8,9},{9,10},{10,1... | collective-permute-start | bytes 14264 | tf_op jit(solution)/shard_map/ppermute | solution.py:17
  74.4 0.9 %copy-start = (f32[5,6,18,130]{3,2,1,0:T(8,128)}, f32[5,6,18,130]{3,2,1,0:T(8,128)S(1)}, u32[]{:S(2)}) copy-start(f32[5,6,18,130]{3,2,1,0:T(8,128)S(1)} %get-tuple-element.46) | copy-start | bytes 842404
  74.7 0.6 copy-start.3
  75.4 0.9 %copy-start.4 = (f32[5,16,128]{2,1,0:T(8,128)S(1)}, f32[5,16,128]{2,1,0:T(8,128)}, u32[]{:S(2)}) copy-start(f32[5,16,128]{2,1,0:T(8,128)} %copy-done.3) | copy-start | bytes 122884
  75.4 0.9 %slice-start = ((f32[5,16,128]{2,1,0:T(8,128)}), f32[3,16,128]{2,1,0:T(8,128)S(1)}, s32[]{:S(2)}) async-start(f32[5,16,128]{2,1,0:T(8,128)} %copy-done.3), calls=%async_computation | async-start | bytes 49152 | tf_op jit(solution)/shard_map/slice | solution.py:151
  75.9 1.1 %copy-start.1 = (f32[5,6,18,130]{3,2,1,0:T(8,128)S(1)}, f32[5,6,18,130]{3,2,1,0:T(8,128)}, u32[]{:S(2)}) copy-start(f32[5,6,18,130]{3,2,1,0:T(8,128)} %copy-done) | copy-start | bytes 842404
where the time goes:
time: 79.8 us; the launch traced here: 79.4 us
  starting transfers between devices  43.1 us (54%)
  waiting for transfers between devices  22.4 us (28%)
  other arithmetic  6.92 us (9%)
  local copies, waits for them, and re-layouts  5.96 us (7%)
  between operations  1.05 us (1%)
    ppermute x3, starting transfers between devices, padded_2(): lax.ppermute(head, axis, [((i + 1) % count, i) for i in range(count)])  23.6 us
    ppermute x3, starting transfers between devices, padded_2(): lax.ppermute(tail, axis, [(i, (i + 1) % count) for i in range(count)])  19.6 us
    ppermute x3, waiting for transfers between devices, padded_2(): lax.ppermute(head, axis, [((i + 1) % count, i) for i in range(count)])  11.7 us
    ppermute x3, waiting for transfers between devices, padded_2(): lax.ppermute(tail, axis, [(i, (i + 1) % count) for i in range(count)])  10.7 us
    unnamed x16, local copies, waits for them, and re-layouts  3.12 us
  transfers between devices with their start and end apart: 6, of which 4 were waited for; matrix products, arithmetic and copies ran while one was open for 1% of the time, Pallas kernels for 0%

commit v1 on v0

v1 whole, which is shorter than its diff:
```python
import jax
import jax.numpy as jnp
from jax import lax
from jax.experimental import pallas as pl
from jax.experimental.pallas import tpu as pltpu
from jax.sharding import PartitionSpec as P

MESH = pl.DeviceIdType.MESH
STEP = 0.05
QUARTER = 0.0125
GAMMA = 5.0 / 3.0

ROW_UP, ROW_DOWN, FACE_R, PACK_UP, PACK_DOWN, TH_UP, TH_DOWN, FACE_T = range(8)
CORNER_UP, CORNER_DOWN, PAIR_UP, PAIR_DOWN, LOW_UP, LOW_DOWN, HIGH_UP, HIGH_DOWN = range(8, 16)
DIRECT = 16


def cell_state(w):
    density, v0, v1, v2, pressure, b0, b1, b2 = w
    kinetic = 0.5 * density * (v0 * v0 + v1 * v1 + v2 * v2)
    magnetic_sq = b0 * b0 + b1 * b1 + b2 * b2
    energy = pressure / (GAMMA - 1.0) + kinetic + 0.5 * magnetic_sq
    conserved = [density, density * v0, density * v1, density * v2, energy]
    return conserved, magnetic_sq


def flux(w, conserved, magnetic_sq, direction):
    density, v0, v1, v2, pressure, b0, b1, b2 = w
    velocity = (v0, v1, v2)
    magnetic = (b0, b1, b2)
    moving = velocity[direction]
    normal = magnetic[direction]
    total_press = pressure + 0.5 * magnetic_sq
    alignment = v0 * b0 + v1 * b1 + v2 * b2
    fast = jnp.sqrt((GAMMA * pressure + magnetic_sq) / density)
    out = [conserved[direction + 1]]
    for component in range(3):
        moment = conserved[component + 1] * moving - magnetic[component] * normal
        if component == direction:
            moment = moment + total_press
        out.append(moment)
    out.append((conserved[4] + total_press) * moving - normal * alignment)
    return out, jnp.abs(moving) + fast


def quantities(w, direction):
    conserved, magnetic_sq = cell_state(w)
    fluxes, speed = flux(w, conserved, magnetic_sq, direction)
    return conserved, fluxes, speed


def face_flux(lower, upper):
    u_low, f_low, s_low = lower
    u_up, f_up, s_up = upper
    half = 0.5 * jnp.maximum(s_low, s_up)
    return [0.5 * (f_low[i] + f_up[i]) - half * (u_up[i] - u_low[i]) for i in range(5)]


def emf(w, component):
    a, b = ((2, 3), (3, 1), (1, 2))[component]
    return -(w[a] * w[b + 4] - w[b] * w[a + 4])


def kernel(
    cells_hbm, faces_hbm, state, faces_new,
    cv, fv, rlo, rhi, f0hi, packs, gp, th_src, gt, f1_src, f1hi, cr_src, cr, pr, e1_own, e1_src, e1f,
    load_sem, send_sem, recv_sem, sem_two, sem_four,
):
    row = lax.axis_index("row")
    th = lax.axis_index("th")
    ph = lax.axis_index("ph")
    rows, ths, phs = lax.axis_size("row"), lax.axis_size("th"), lax.axis_size("ph")
    z = th * phs + ph
    depth = ths * phs
    at_bottom, at_top = row == 0, row == rows - 1
    at_north, at_south = th == 0, th == ths - 1
    first_z = z == 0
    far_sender = (z == phs - 1) | (z == phs) | (z == phs + 1) | (z == 2 * phs - 1)

    def at_z(place):
        return {"row": row, "th": place // phs, "ph": lax.rem(place, phs)}

    def place(dr=0, dt=0, dp=0):
        return {"row": row + dr, "th": th + dt, "ph": lax.rem(ph + dp + phs, phs)}

    barrier = pltpu.get_barrier_semaphore()

    def tell(semaphore, condition, target):
        @pl.when(condition)
        def _():
            pl.semaphore_signal(semaphore, inc=1, device_id=target, device_id_type=MESH)

    for far in (phs - 1, phs, phs + 1, 2 * phs - 1):
        tell(barrier, first_z, {"row": row, "th": far // phs, "ph": far % phs})
    tell(barrier, row < rows - 1, place(dr=1))
    tell(barrier, row > 0, place(dr=-1))
    for hop in (1, 2):
        tell(barrier, z + hop < depth, at_z(z + hop))
        tell(barrier, z - hop >= 0, at_z(z - hop))

    load_cells = pltpu.make_async_copy(cells_hbm, cv, load_sem.at[0])
    load_faces = pltpu.make_async_copy(faces_hbm, fv, load_sem.at[1])
    load_cells.start()
    load_faces.start()

    def copy(kind, src, dst, target, recv=None):
        return pltpu.make_async_remote_copy(
            src_ref=src, dst_ref=dst, send_sem=send_sem.at[kind],
            recv_sem=recv_sem.at[kind if recv is None else recv],
            device_id=target, device_id_type=MESH,
        )

    up_r, down_r = place(dr=1), place(dr=-1)
    up_t, down_t = place(dt=1), place(dt=-1)
    up_p, down_p = place(dp=1), place(dp=-1)
    origin = {"row": row, "th": th * 0, "ph": ph * 0}
    copies = {
        ROW_UP: copy(ROW_UP, cv.at[:, 3], rlo, up_r),
        ROW_DOWN: copy(ROW_DOWN, cv.at[:, 0], rhi, down_r),
        FACE_R: copy(FACE_R, fv.at[0, 0], f0hi, down_r),
        PACK_UP: copy(PACK_UP, packs.at[1], gp.at[0], up_p),
        PACK_DOWN: copy(PACK_DOWN, packs.at[0], gp.at[1], down_p),
        TH_UP: copy(TH_UP, th_src.at[1], gt.at[0], up_t),
        TH_DOWN: copy(TH_DOWN, th_src.at[0], gt.at[1], down_t),
        FACE_T: copy(FACE_T, f1_src, f1hi, down_t),
        CORNER_UP: copy(CORNER_UP, cr_src.at[1], cr.at[0], up_t),
        CORNER_DOWN: copy(CORNER_DOWN, cr_src.at[0], cr.at[1], down_t),
        PAIR_UP: copy(PAIR_UP, gp, pr.at[0], up_r),
        PAIR_DOWN: copy(PAIR_DOWN, gp, pr.at[1], down_r),
        LOW_UP: copy(LOW_UP, e1_src.at[0], e1f.at[0, 0], up_p),
        LOW_DOWN: copy(LOW_DOWN, e1_src.at[0], e1f.at[1, 0], down_p),
        HIGH_UP: copy(HIGH_UP, e1_src.at[1], e1f.at[0, 1], up_p),
        HIGH_DOWN: copy(HIGH_DOWN, e1_src.at[1], e1f.at[1, 1], down_p),
    }
    direct_left = copy(DIRECT, e1_own, e1f.at[0, 1], origin, HIGH_UP)
    direct_right = copy(DIRECT, e1_own, e1f.at[1, 1], origin, HIGH_DOWN)

    def send(kind, condition=None):
        if condition is None:
            copies[kind].start()
        else:
            pl.when(condition)(copies[kind].start)

    def arrived(kind, condition=None):
        if condition is None:
            copies[kind].wait_recv()
        else:
            pl.when(condition)(copies[kind].wait_recv)

    load_cells.wait()
    for r in range(4):
        w = [cv[f, r, 0:1] for f in range(8)]
        e1_own[r : r + 1] = emf(w, 0)
        for f in range(8):
            th_src[0, f * 4 + r : f * 4 + r + 1] = w[f]
            th_src[1, f * 4 + r : f * 4 + r + 1] = cv[f, r, 15:16]
    load_faces.wait()
    for r in range(4):
        f1_src[r : r + 1] = fv[1, r, 0:1]
    for c in range(4):
        turned = cv[2 * c : 2 * c + 2].reshape(128, 128).T
        packs[0, c : c + 1] = turned[0:1]
        packs[1, c : c + 1] = turned[127:128]
    third = fv[2].reshape(64, 128)
    turned = jnp.concatenate([third, third], axis=0).T
    for c in range(4, 8):
        packs[0, c : c + 1] = turned[0:1]
        packs[1, c : c + 1] = turned[127:128]

    @pl.when(at_bottom)
    def _():
        rlo[...] = cv[:, 0]

    @pl.when(at_top)
    def _():
        rhi[...] = cv[:, 3]
        f0hi[...] = fv[0, 3]

    def fill_polar(side, condition):
        @pl.when(condition)
        def _():
            for f in range(8):
                rows_f = th_src[side, f * 4 : f * 4 + 4]
                gt[side, f * 4 : f * 4 + 4] = -rows_f if f in (2, 7) else rows_f

    fill_polar(0, at_north)
    fill_polar(1, at_south)

    def ghost_rows(side):
        return [gt[side, f * 4 : f * 4 + 4] for f in range(8)]

    @pl.when(at_north)
    def _():
        e1_src[0] = emf(ghost_rows(0), 0)

    count = (
        (z >= 1).astype(jnp.int32) + (z >= 2).astype(jnp.int32)
        + (z < depth - 1).astype(jnp.int32) + (z < depth - 2).astype(jnp.int32)
        + (row > 0).astype(jnp.int32) + (row < rows - 1).astype(jnp.int32)
        + far_sender.astype(jnp.int32)
    )
    pl.semaphore_wait(barrier, count)

    pl.when(z == 2 * phs - 1)(direct_left.start)
    pl.when(z == phs + 1)(direct_right.start)
    tell(sem_two, z + 2 < depth, at_z(z + 2))
    tell(sem_two, z - 2 >= 0, at_z(z - 2))
    early_down = z == phs
    send(TH_DOWN, early_down)
    send(FACE_T, early_down)
    near_up = (ph < phs - 1) | (z == phs - 1)
    near_down = ph > 0
    send(PACK_UP, near_up)
    send(PACK_DOWN, near_down)
    send(LOW_UP, at_north & near_up)
    send(LOW_DOWN, at_north & near_down)
    send(ROW_UP, row < rows - 1)
    send(ROW_DOWN, row > 0)
    send(FACE_R, row > 0)

    two = (z >= 2).astype(jnp.int32) + (z < depth - 2).astype(jnp.int32)
    pl.semaphore_wait(sem_two, two)
    tell(sem_four, z + 4 < depth, at_z(z + 4))
    tell(sem_four, z - 4 >= 0, at_z(z - 4))

    arrived(ROW_UP, row > 0)
    arrived(ROW_DOWN, row < rows - 1)
    arrived(FACE_R, row < rows - 1)
    for side, line in ((0, 0), (1, 15)):
        for k, ghost in enumerate((rlo, rhi)):
            w = [ghost[f, line : line + 1] for f in range(8)]
            cr_src[side, k : k + 1] = emf(w, 2)

    def fill_corner(side, line, condition):
        @pl.when(condition)
        def _():
            for k, ghost in enumerate((rlo, rhi)):
                w = [ghost[f, line : line + 1] for f in range(8)]
                w[2] = -w[2]
                cr[side, k : k + 1] = emf(w, 2)

    fill_corner(0, 0, at_north)
    fill_corner(1, 15, at_south)
    send(CORNER_DOWN, early_down)

    four = (z >= 4).astype(jnp.int32) + (z < depth - 4).astype(jnp.int32)
    pl.semaphore_wait(sem_four, four)

    later_down = (th > 0) & jnp.logical_not(early_down)
    send(TH_UP, th < ths - 1)
    send(TH_DOWN, later_down)
    send(FACE_T, later_down)
    send(PACK_UP, jnp.logical_not(near_up))
    send(PACK_DOWN, jnp.logical_not(near_down))
    send(LOW_DOWN, at_north & jnp.logical_not(near_down))
    send(CORNER_UP, th < ths - 1)
    send(CORNER_DOWN, later_down)

    shape = (4, 16, 128)
    lane = lax.broadcasted_iota(jnp.int32, shape, 2)
    line = lax.broadcasted_iota(jnp.int32, shape, 1)
    own = [cv[f] for f in range(8)]

    def ahead_t(x):
        return pltpu.roll(x, 15, 1)

    def behind_t(x):
        return pltpu.roll(x, 1, 1)

    def ahead_p(x):
        return pltpu.roll(x, 127, 2)

    def behind_p(x):
        return pltpu.roll(x, 1, 2)

    low = quantities([rlo[f][None] for f in range(8)], 0)
    mid = quantities(own, 0)
    high = quantities([rhi[f][None] for f in range(8)], 0)

    def tall(a, b, c):
        return jnp.concatenate([a, b, c], axis=0)

    u6 = [tall(low[0][i], mid[0][i], high[0][i]) for i in range(5)]
    g6 = [tall(low[1][i], mid[1][i], high[1][i]) for i in range(5)]
    s6 = tall(low[2], mid[2], high[2])
    face = face_flux(([u[:-1] for u in u6], [g[:-1] for g in g6], s6[:-1]), ([u[1:] for u in u6], [g[1:] for g in g6], s6[1:]))
    for i in range(5):
        state[i] = mid[0][i] - STEP * (face[i][1:] - face[i][:-1])

    arrived(PACK_DOWN)
    arrived(PACK_UP)
    send(PAIR_UP, row < rows - 1)
    send(PAIR_DOWN, row > 0)
    columns = jnp.concatenate([gp[0], gp[1]], axis=0).T

    def column(side, c, half):
        col = columns[half * 64 : half * 64 + 64, side * 8 + c : side * 8 + c + 1]
        return jnp.broadcast_to(col, (64, 128)).reshape(shape)

    left, right = lane == 0, lane == 127
    beside = [
        jnp.where(left, column(0, f // 2, f % 2), jnp.where(right, column(1, f // 2, f % 2), own[f]))
        for f in range(8)
    ]
    upper_third = column(1, 4, 0)
    e1_beside, e2_beside = emf(beside, 0), emf(beside, 1)

    def apply(direction, outer, ahead, behind, is_low, is_high):
        mine = quantities(own, direction)
        edge = quantities(outer, direction)

        def shifted(a, b):
            return jnp.where(is_high, b, ahead(a))

        above = (
            [shifted(mine[0][i], edge[0][i]) for i in range(5)],
            [shifted(mine[1][i], edge[1][i]) for i in range(5)],
            shifted(mine[2], edge[2]),
        )
        upper = face_flux(mine, above)
        lower = face_flux(edge, mine)
        for i in range(5):
            below = jnp.where(is_low, lower[i], behind(upper[i]))
            state[i] = state[i] - STEP * (upper[i] - below)

    apply(2, beside, ahead_p, behind_p, left, right)

    arrived(TH_UP, th > 0)

    @pl.when(th > 0)
    def _():
        e1_src[0] = emf(ghost_rows(0), 0)

    send(LOW_UP, th > 0)
    send(LOW_DOWN, th > 0)
    arrived(TH_DOWN, th < ths - 1)
    arrived(FACE_T, th < ths - 1)
    e1_src[1] = emf(ghost_rows(1), 0)
    send(HIGH_UP, z != phs - 1)
    send(HIGH_DOWN, z != 1)

    north, south = line == 0, line == 15

    def spread(ref, *index):
        return jnp.concatenate([jnp.broadcast_to(ref[index + (slice(start, start + 1),)], (16, 128))[None] for start in spread.rows], axis=0)

    def polar(f):
        spread.rows = [f * 4 + r for r in range(4)]
        return jnp.where(north, spread(gt, 0), jnp.where(south, spread(gt, 1), own[f]))

    outside = [polar(f) for f in range(8)]
    apply(1, outside, ahead_t, behind_t, north, south)
    e1_outside, e3_outside = emf(outside, 0), emf(outside, 2)

    arrived(CORNER_UP, th > 0)
    arrived(CORNER_DOWN, th < ths - 1)
    arrived(PAIR_UP, row > 0)
    arrived(PAIR_DOWN, row < rows - 1)

    def pair_emf(ref, *index):
        rows8 = ref[index] if index else ref[...]
        return -(rows8[1:2] * rows8[2:3] - rows8[0:1] * rows8[3:4])

    pair_rows = [pair_emf(gp, 0), pair_emf(gp, 1), pair_emf(pr, 0, 0), pair_emf(pr, 0, 1), pair_emf(pr, 1, 0), pair_emf(pr, 1, 1)]
    pair_columns = jnp.concatenate(pair_rows + [pair_rows[0], pair_rows[0]], axis=0).T

    def pair_ghost(side):
        lanes = lane[:1]
        parts = []
        for k in range(2):
            near = pair_columns[64:80, k : k + 1] if side == 0 else pair_columns[112:128, k : k + 1]
            far_col = pair_columns[112:128, 2 + k : 3 + k] if side == 0 else pair_columns[64:80, 4 + k : 5 + k]
            edge = at_bottom if side == 0 else at_top
            parts.append(jnp.broadcast_to(jnp.where(edge, near, far_col), (16, 128))[None])
        return jnp.where(lanes == 0, parts[0], parts[1])

    def corner_ghost(k):
        a = jnp.broadcast_to(cr[0, k : k + 1], (16, 128))[None]
        b = jnp.broadcast_to(cr[1, k : k + 1], (16, 128))[None]
        return jnp.where(line[:1] == 0, a, b)

    low_w = [rlo[f][None] for f in range(8)]
    high_w = [rhi[f][None] for f in range(8)]
    e1 = emf(own, 0)
    e2 = tall(emf(low_w, 1), emf(own, 1), emf(high_w, 1))
    e3 = tall(emf(low_w, 2), emf(own, 2), emf(high_w, 2))
    e2_side = tall(pair_ghost(0), e2_beside, pair_ghost(1))
    e3_side = tall(corner_ghost(0), e3_outside, corner_ghost(1))

    six = (6, 16, 128)
    lane6 = lax.broadcasted_iota(jnp.int32, six, 2)
    line6 = lax.broadcasted_iota(jnp.int32, six, 1)
    across_t = jnp.where(line6 == 15, e3_side, ahead_t(e3)) - jnp.where(line6 == 0, e3_side, behind_t(e3))
    across_p = jnp.where(lane6 == 127, e2_side, ahead_p(e2)) - jnp.where(lane6 == 0, e2_side, behind_p(e2))
    curl = across_t - across_p
    new_first = fv[0] - QUARTER * (curl[:4] + curl[1:5])
    new_last = f0hi[...] - QUARTER * (curl[4] + curl[5])
    faces_new[0] = new_first
    last = jnp.where(at_top, new_first[3], new_last)
    state[5] = 0.5 * (new_first + jnp.concatenate([new_first[1:], last[None]], axis=0))

    zero = jnp.zeros(shape, jnp.float32)
    curl = (e2[2:] - e2[:-2]) - (
        jnp.where(south, e1_outside, ahead_t(e1)) - jnp.where(north, e1_outside, behind_t(e1))
    )
    curl_beside = (e2_side[2:] - e2_side[:-2]) - (
        jnp.where(south, zero, ahead_t(e1_beside)) - jnp.where(north, zero, behind_t(e1_beside))
    )
    new_third = fv[2] - QUARTER * (curl + jnp.where(left, curl_beside, behind_p(curl)))
    new_upper = upper_third - QUARTER * (curl + curl_beside)
    faces_new[2] = new_third
    state[7] = 0.5 * (new_third + jnp.where(right, new_upper, ahead_p(new_third)))

    curl = (
        jnp.where(right, e1_beside, ahead_p(e1)) - jnp.where(left, e1_beside, behind_p(e1))
    ) - (e3[2:] - e3[:-2])
    curl_outside = (
        jnp.where(right, zero, ahead_p(e1_outside)) - jnp.where(left, zero, behind_p(e1_outside))
    ) - (e3_side[2:] - e3_side[:-2])
    new_second = fv[1] - QUARTER * (curl + jnp.where(north, curl_outside, behind_t(curl)))
    spread.rows = [0, 1, 2, 3]
    new_upper = spread(f1hi) - QUARTER * (curl + curl_outside)
    new_upper = jnp.where(at_south, 0.0, new_upper)
    faces_new[1] = new_second
    state[6] = 0.5 * (new_second + jnp.where(south, new_upper, ahead_t(new_second)))

    arrived(LOW_UP)
    arrived(LOW_DOWN)
    arrived(HIGH_DOWN)
    arrived(HIGH_UP)
    lane4 = lax.broadcasted_iota(jnp.int32, (4, 128), 1)

    def corner_rows(k):
        a = jnp.where(lane4 == 0, pltpu.roll(e1f[0, k], 1, 1), 0.0)
        b = jnp.where(lane4 == 127, pltpu.roll(e1f[1, k], 127, 1), 0.0)
        return QUARTER * a, QUARTER * b

    a_low, b_low = corner_rows(0)
    a_high, b_high = corner_rows(1)
    keep = jnp.where(at_south, 0.0, 0.5)
    for r in range(4):
        a, b = a_low[r : r + 1], b_low[r : r + 1]
        faces_new[1, r, 0:1] = faces_new[1, r, 0:1] - (b - a)
        state[6, r, 0:1] = state[6, r, 0:1] - 0.5 * (b - a)
        faces_new[2, r, 0:1] = faces_new[2, r, 0:1] - a
        state[7, r, 0:1] = state[7, r, 0:1] - 0.5 * (a + b)
        a, b = a_high[r : r + 1], b_high[r : r + 1]
        state[6, r, 15:16] = state[6, r, 15:16] - keep * (b - a)
        faces_new[2, r, 15:16] = faces_new[2, r, 15:16] + a
        state[7, r, 15:16] = state[7, r, 15:16] + 0.5 * (a + b)

    for kind, condition in (
        (ROW_UP, row < rows - 1), (ROW_DOWN, row > 0), (FACE_R, row > 0), (PACK_UP, None), (PACK_DOWN, None),
        (TH_UP, th < ths - 1), (TH_DOWN, th > 0), (FACE_T, th > 0), (CORNER_UP, th < ths - 1), (CORNER_DOWN, th > 0),
        (PAIR_UP, row < rows - 1), (PAIR_DOWN, row > 0), (LOW_UP, None), (LOW_DOWN, None),
        (HIGH_UP, z != phs - 1), (HIGH_DOWN, z != 1),
    ):
        if condition is None:
            copies[kind].wait_send()
        else:
            pl.when(condition)(copies[kind].wait_send)
    pl.when(z == 2 * phs - 1)(direct_left.wait_send)
    pl.when(z == phs + 1)(direct_right.wait_send)


def on_device(cells, faces):
    f32 = jnp.float32
    return pl.pallas_call(
        kernel,
        out_shape=(jax.ShapeDtypeStruct((8, 4, 16, 128), f32), jax.ShapeDtypeStruct((3, 4, 16, 128), f32)),
        in_specs=[pl.BlockSpec(memory_space=pl.ANY)] * 2,
        out_specs=(pl.BlockSpec(memory_space=pltpu.VMEM),) * 2,
        scratch_shapes=[
            pltpu.VMEM((8, 4, 16, 128), f32),
            pltpu.VMEM((3, 4, 16, 128), f32),
            pltpu.VMEM((8, 16, 128), f32),
            pltpu.VMEM((8, 16, 128), f32),
            pltpu.VMEM((16, 128), f32),
            pltpu.VMEM((2, 8, 128), f32),
            pltpu.VMEM((2, 8, 128), f32),
            pltpu.VMEM((2, 32, 128), f32),
            pltpu.VMEM((2, 32, 128), f32),
            pltpu.VMEM((4, 128), f32),
            pltpu.VMEM((4, 128), f32),
            pltpu.VMEM((2, 2, 128), f32),
            pltpu.VMEM((2, 2, 128), f32),
            pltpu.VMEM((2, 2, 8, 128), f32),
            pltpu.VMEM((4, 128), f32),
            pltpu.VMEM((2, 4, 128), f32),
            pltpu.VMEM((2, 2, 4, 128), f32),
            pltpu.SemaphoreType.DMA((2,)),
            pltpu.SemaphoreType.DMA((17,)),
            pltpu.SemaphoreType.DMA((17,)),
            pltpu.SemaphoreType.REGULAR,
            pltpu.SemaphoreType.REGULAR,
        ],
        name="section",
        compiler_params=pltpu.CompilerParams(collective_id=0, has_side_effects=True),
    )(cells, faces)


def solution(mesh):
    spec = P(None, "row", "th", "ph")
    return jax.shard_map(on_device, mesh=mesh, in_specs=(spec, spec), out_specs=(spec, spec), check_vma=False)
```

time: 79.8 us -> 39.3 us (0.49)
  the two profiles are of different devices: /device:TPU:6 before, /device:TPU:64 now
where the time goes in v1:
time: 39.3 us; the launch traced here: 39.1 us
  Pallas kernels  36.1 us (92%)
  local copies, waits for them, and re-layouts  2.35 us (6%)
  between operations  0.65 us (2%)
    pallas_call x1, Pallas kernels, on_device(): pl.pallas_call(kernel, out_shape=(jax.ShapeDtypeStruct((8, 4, 16, 128), f...  36.1 us
    unnamed x4, local copies, waits for them, and re-layouts  2.35 us

profile of v1, /device:TPU:64, one launch (start us, length us, event | category | flops | bytes accessed | tf_op | source)
XLA Modules:
  0.0 39.1 jit_solution(7711595871389849751)
XLA Ops:
  0.6 36.1 %section.1 = (f32[8,4,16,128]{3,2,1,0:T(8,128)}, f32[3,4,16,128]{3,2,1,0:T(8,128)}) custom-call(f32[8,4,16,128]{3,2,1,0:T(8,128)} %cells_hbm.1, f32[3,4,16,128]{3,2,1,0:T(8,128)} %faces_hbm.1), custom_call_target="tpu_custom_call" | custom-call | tf_op jit(solution)/shard_map/section/pallas_call | solution.py:468
  36.8 0.0 copy-start
  36.8 1.7 %copy.6 = f32[8,4,16,128]{3,2,1,0:T(8,128)} copy(f32[8,4,16,128]{3,2,1,0:T(8,128)} %get-tuple-element.4) | data formatting | bytes 524288
  38.5 0.0 copy-done
  38.5 0.6 %copy.7 = f32[3,4,16,128]{3,2,1,0:T(8,128)} copy(f32[3,4,16,128]{3,2,1,0:T(8,128)S(1)} %copy-done) | data formatting | bytes 196608
Async XLA Ops:
  36.8 1.7 %copy-start = (f32[3,4,16,128]{3,2,1,0:T(8,128)S(1)}, f32[3,4,16,128]{3,2,1,0:T(8,128)}, u32[]{:S(2)}) copy-start(f32[3,4,16,128]{3,2,1,0:T(8,128)} %get-tuple-element.5) | copy-start | bytes 294916

commit v2 on v1

--- a/solution.py
+++ b/solution.py
@@ -63,8 +63,8 @@
 
 def kernel(
     cells_hbm, faces_hbm, state, faces_new,
-    cv, fv, rlo, rhi, f0hi, packs, gp, th_src, gt, f1_src, f1hi, cr_src, cr, pr, e1_own, e1_src, e1f,
-    load_sem, send_sem, recv_sem, sem_two, sem_four,
+    cv, fv, first_rows, rlo, rhi, f0hi, packs, gp, th_src, gt, f1_src, f1hi, cr_src, cr, pr, e1_own, e1_src, e1f,
+    load_sem, send_sem, recv_sem, ok_near, ok_wrap, ok_th,
 ):
     row = lax.axis_index("row")
     th = lax.axis_index("th")
@@ -75,13 +75,23 @@
     at_bottom, at_top = row == 0, row == rows - 1
     at_north, at_south = th == 0, th == ths - 1
     first_z = z == 0
-    far_sender = (z == phs - 1) | (z == phs) | (z == phs + 1) | (z == 2 * phs - 1)
-
-    def at_z(place):
-        return {"row": row, "th": place // phs, "ph": lax.rem(place, phs)}
+    corner_sender = (z == 2 * phs - 1) & (row > 0)
 
     def place(dr=0, dt=0, dp=0):
         return {"row": row + dr, "th": th + dt, "ph": lax.rem(ph + dp + phs, phs)}
+
+    load_cells = pltpu.make_async_copy(cells_hbm, cv, load_sem.at[0])
+    load_faces = pltpu.make_async_copy(faces_hbm, fv, load_sem.at[1])
+    load_velocity = pltpu.make_async_copy(cells_hbm.at[2:4, :, 0:8], first_rows.at[0:2], load_sem.at[2])
+    load_field = pltpu.make_async_copy(cells_hbm.at[6:8, :, 0:8], first_rows.at[2:4], load_sem.at[3])
+
+    @pl.when(corner_sender)
+    def _():
+        load_velocity.start()
+        load_field.start()
+
+    load_cells.start()
+    load_faces.start()
 
     barrier = pltpu.get_barrier_semaphore()
 
@@ -90,18 +100,20 @@
         def _():
             pl.semaphore_signal(semaphore, inc=1, device_id=target, device_id_type=MESH)
 
-    for far in (phs - 1, phs, phs + 1, 2 * phs - 1):
-        tell(barrier, first_z, {"row": row, "th": far // phs, "ph": far % phs})
+    def told(semaphore, condition):
+        @pl.when(condition)
+        def _():
+            pl.semaphore_wait(semaphore, 1)
+
+    has_up, has_down = th < ths - 1, th > 0
+    first_p, last_p = ph == 0, ph == phs - 1
+    inner_up, inner_down = ph < phs - 1, ph > 0
     tell(barrier, row < rows - 1, place(dr=1))
     tell(barrier, row > 0, place(dr=-1))
-    for hop in (1, 2):
-        tell(barrier, z + hop < depth, at_z(z + hop))
-        tell(barrier, z - hop >= 0, at_z(z - hop))
-
-    load_cells = pltpu.make_async_copy(cells_hbm, cv, load_sem.at[0])
-    load_faces = pltpu.make_async_copy(faces_hbm, fv, load_sem.at[1])
-    load_cells.start()
-    load_faces.start()
+    tell(barrier, inner_up, place(dp=1))
+    tell(barrier, has_up, place(dt=1))
+    tell(barrier, first_p, place(dp=-1))
+    tell(barrier, (z == 0) & (row > 0), {"row": row, "th": 1, "ph": phs - 1})
 
     def copy(kind, src, dst, target, recv=None):
         return pltpu.make_async_remote_copy(
@@ -133,7 +145,6 @@
         HIGH_DOWN: copy(HIGH_DOWN, e1_src.at[1], e1f.at[1, 1], down_p),
     }
     direct_left = copy(DIRECT, e1_own, e1f.at[0, 1], origin, HIGH_UP)
-    direct_right = copy(DIRECT, e1_own, e1f.at[1, 1], origin, HIGH_DOWN)
 
     def send(kind, condition=None):
         if condition is None:
@@ -147,23 +158,46 @@
         else:
             pl.when(condition)(copies[kind].wait_recv)
 
+    @pl.when(corner_sender)
+    def _():
+        load_velocity.wait()
+        load_field.wait()
+        for r in range(4):
+            w = [first_rows[k, r, 0:1] for k in range(4)]
+            e1_own[r : r + 1] = -(w[0] * w[3] - w[1] * w[2])
+
+    def number(*conditions):
+        total = jnp.int32(0)
+        for condition in conditions:
+            total = total + condition.astype(jnp.int32)
+        return total
+
+    pl.semaphore_wait(barrier, number(corner_sender, has_down, last_p, row > 0, row < rows - 1, inner_down))
+    pl.when(corner_sender)(direct_left.start)
+    tell(ok_th, has_down, place(dt=-1))
+    tell(ok_wrap, last_p, place(dp=1))
+    tell(ok_near, inner_down, place(dp=-1))
+
     load_cells.wait()
+    send(ROW_UP, row < rows - 1)
+    send(ROW_DOWN, row > 0)
     for r in range(4):
-        w = [cv[f, r, 0:1] for f in range(8)]
-        e1_own[r : r + 1] = emf(w, 0)
         for f in range(8):
-            th_src[0, f * 4 + r : f * 4 + r + 1] = w[f]
+            th_src[0, f * 4 + r : f * 4 + r + 1] = cv[f, r, 0:1]
             th_src[1, f * 4 + r : f * 4 + r + 1] = cv[f, r, 15:16]
     load_faces.wait()
+    send(FACE_R, row > 0)
     for r in range(4):
         f1_src[r : r + 1] = fv[1, r, 0:1]
-    for c in range(4):
-        turned = cv[2 * c : 2 * c + 2].reshape(128, 128).T
-        packs[0, c : c + 1] = turned[0:1]
-        packs[1, c : c + 1] = turned[127:128]
     third = fv[2].reshape(64, 128)
     turned = jnp.concatenate([third, third], axis=0).T
     for c in range(4, 8):
+        packs[0, c : c + 1] = turned[0:1]
+        packs[1, c : c + 1] = turned[127:128]
+    send(TH_DOWN, has_down)
+    send(FACE_T, has_down)
+    for c in range(4):
+        turned = cv[2 * c : 2 * c + 2].reshape(128, 128).T
         packs[0, c : c + 1] = turned[0:1]
         packs[1, c : c + 1] = turned[127:128]
 
@@ -193,35 +227,10 @@
     def _():
         e1_src[0] = emf(ghost_rows(0), 0)
 
-    count = (
-        (z >= 1).astype(jnp.int32) + (z >= 2).astype(jnp.int32)
-        + (z < depth - 1).astype(jnp.int32) + (z < depth - 2).astype(jnp.int32)
-        + (row > 0).astype(jnp.int32) + (row < rows - 1).astype(jnp.int32)
-        + far_sender.astype(jnp.int32)
-    )
-    pl.semaphore_wait(barrier, count)
-
-    pl.when(z == 2 * phs - 1)(direct_left.start)
-    pl.when(z == phs + 1)(direct_right.start)
-    tell(sem_two, z + 2 < depth, at_z(z + 2))
-    tell(sem_two, z - 2 >= 0, at_z(z - 2))
-    early_down = z == phs
-    send(TH_DOWN, early_down)
-    send(FACE_T, early_down)
-    near_up = (ph < phs - 1) | (z == phs - 1)
-    near_down = ph > 0
-    send(PACK_UP, near_up)
-    send(PACK_DOWN, near_down)
-    send(LOW_UP, at_north & near_up)
-    send(LOW_DOWN, at_north & near_down)
-    send(ROW_UP, row < rows - 1)
-    send(ROW_DOWN, row > 0)
-    send(FACE_R, row > 0)
-
-    two = (z >= 2).astype(jnp.int32) + (z < depth - 2).astype(jnp.int32)
-    pl.semaphore_wait(sem_two, two)
-    tell(sem_four, z + 4 < depth, at_z(z + 4))
-    tell(sem_four, z - 4 >= 0, at_z(z - 4))
+    send(PACK_DOWN, inner_down)
+    send(PACK_UP, last_p)
+    send(LOW_DOWN, at_north & inner_down)
+    send(LOW_UP, at_north & last_p)
 
     arrived(ROW_UP, row > 0)
     arrived(ROW_DOWN, row < rows - 1)
@@ -241,20 +250,11 @@
 
     fill_corner(0, 0, at_north)
     fill_corner(1, 15, at_south)
-    send(CORNER_DOWN, early_down)
-
-    four = (z >= 4).astype(jnp.int32) + (z < depth - 4).astype(jnp.int32)
-    pl.semaphore_wait(sem_four, four)
-
-    later_down = (th > 0) & jnp.logical_not(early_down)
-    send(TH_UP, th < ths - 1)
-    send(TH_DOWN, later_down)
-    send(FACE_T, later_down)
-    send(PACK_UP, jnp.logical_not(near_up))
-    send(PACK_DOWN, jnp.logical_not(near_down))
-    send(LOW_DOWN, at_north & jnp.logical_not(near_down))
-    send(CORNER_UP, th < ths - 1)
-    send(CORNER_DOWN, later_down)
+    send(CORNER_DOWN, has_down)
+
+    told(ok_near, inner_up)
+    send(PACK_UP, inner_up)
+    send(LOW_UP, at_north & inner_up)
 
     shape = (4, 16, 128)
     lane = lax.broadcasted_iota(jnp.int32, shape, 2)
@@ -286,6 +286,17 @@
     face = face_flux(([u[:-1] for u in u6], [g[:-1] for g in g6], s6[:-1]), ([u[1:] for u in u6], [g[1:] for g in g6], s6[1:]))
     for i in range(5):
         state[i] = mid[0][i] - STEP * (face[i][1:] - face[i][:-1])
+
+    told(ok_wrap, first_p)
+    send(PACK_DOWN, first_p)
+    send(LOW_DOWN, at_north & first_p)
+
+    def send_up(condition):
+        told(ok_th, condition)
+        send(TH_UP, condition)
+        send(CORNER_UP, condition)
+
+    send_up(has_up & last_p)
 
     arrived(PACK_DOWN)
     arrived(PACK_UP)
@@ -324,6 +335,7 @@
             state[i] = state[i] - STEP * (upper[i] - below)
 
     apply(2, beside, ahead_p, behind_p, left, right)
+    send_up(has_up & jnp.logical_not(last_p))
 
     arrived(TH_UP, th > 0)
 
@@ -336,8 +348,9 @@
     arrived(TH_DOWN, th < ths - 1)
     arrived(FACE_T, th < ths - 1)
     e1_src[1] = emf(ghost_rows(1), 0)
-    send(HIGH_UP, z != phs - 1)
-    send(HIGH_DOWN, z != 1)
+    high_up = (z != phs - 1) | (row == 0)
+    send(HIGH_UP, high_up)
+    send(HIGH_DOWN)
 
     north, south = line == 0, line == 15
 
@@ -453,26 +466,38 @@
         (ROW_UP, row < rows - 1), (ROW_DOWN, row > 0), (FACE_R, row > 0), (PACK_UP, None), (PACK_DOWN, None),
         (TH_UP, th < ths - 1), (TH_DOWN, th > 0), (FACE_T, th > 0), (CORNER_UP, th < ths - 1), (CORNER_DOWN, th > 0),
         (PAIR_UP, row < rows - 1), (PAIR_DOWN, row > 0), (LOW_UP, None), (LOW_DOWN, None),
-        (HIGH_UP, z != phs - 1), (HIGH_DOWN, z != 1),
+        (HIGH_UP, high_up), (HIGH_DOWN, None),
     ):
         if condition is None:
             copies[kind].wait_send()
         else:
             pl.when(condition)(copies[kind].wait_send)
-    pl.when(z == 2 * phs - 1)(direct_left.wait_send)
-    pl.when(z == phs + 1)(direct_right.wait_send)
+    pl.when(corner_sender)(direct_left.wait_send)
+
+
+def write_out(state, faces_new, state_hbm, faces_hbm, sem):
+    copies = [
+        pltpu.make_async_copy(state, state_hbm, sem.at[0]),
+        pltpu.make_async_copy(faces_new, faces_hbm, sem.at[1]),
+    ]
+    for copy in copies:
+        copy.start()
+    for copy in copies:
+        copy.wait()
 
 
 def on_device(cells, faces):
     f32 = jnp.float32
-    return pl.pallas_call(
+    shapes = ((8, 4, 16, 128), (3, 4, 16, 128))
+    outputs = pl.pallas_call(
         kernel,
-        out_shape=(jax.ShapeDtypeStruct((8, 4, 16, 128), f32), jax.ShapeDtypeStruct((3, 4, 16, 128), f32)),
+        out_shape=tuple(pltpu.VMEM(shape, f32) for shape in shapes),
         in_specs=[pl.BlockSpec(memory_space=pl.ANY)] * 2,
         out_specs=(pl.BlockSpec(memory_space=pltpu.VMEM),) * 2,
         scratch_shapes=[
             pltpu.VMEM((8, 4, 16, 128), f32),
             pltpu.VMEM((3, 4, 16, 128), f32),
+            pltpu.VMEM((4, 4, 8, 128), f32),
             pltpu.VMEM((8, 16, 128), f32),
             pltpu.VMEM((8, 16, 128), f32),
             pltpu.VMEM((16, 128), f32),
@@ -488,15 +513,24 @@
             pltpu.VMEM((4, 128), f32),
             pltpu.VMEM((2, 4, 128), f32),
             pltpu.VMEM((2, 2, 4, 128), f32),
-            pltpu.SemaphoreType.DMA((2,)),
+            pltpu.SemaphoreType.DMA((4,)),
             pltpu.SemaphoreType.DMA((17,)),
             pltpu.SemaphoreType.DMA((17,)),
+            pltpu.SemaphoreType.REGULAR,
             pltpu.SemaphoreType.REGULAR,
             pltpu.SemaphoreType.REGULAR,
         ],
         name="section",
         compiler_params=pltpu.CompilerParams(collective_id=0, has_side_effects=True),
     )(cells, faces)
+    return pl.pallas_call(
+        write_out,
+        out_shape=tuple(jax.ShapeDtypeStruct(shape, f32) for shape in shapes),
+        in_specs=[pl.BlockSpec(memory_space=pltpu.VMEM)] * 2,
+        out_specs=(pl.BlockSpec(memory_space=pl.ANY),) * 2,
+        scratch_shapes=[pltpu.SemaphoreType.DMA((2,))],
+        name="write_out",
+    )(*(pltpu.with_memory_space_constraint(x, pltpu.VMEM) for x in outputs))
 
 
 def solution(mesh):

time: 39.3 us -> 31.5 us (0.80)
  the two profiles are of different devices: /device:TPU:64 before, /device:TPU:6 now
where the time goes in v2:
time: 31.5 us; the launch traced here: 31.4 us
  Pallas kernels  30.7 us (97%)
  between operations  0.64 us (2%)
    pallas_call x1, Pallas kernels, on_device(): pl.pallas_call(kernel, out_shape=tuple((pltpu.VMEM(shape, f32) for shape...  30 us
    pallas_call x1, Pallas kernels, on_device(): pl.pallas_call(write_out, out_shape=tuple((jax.ShapeDtypeStruct(shape, f3...  0.75 us

profile of v2, /device:TPU:6, one launch (start us, length us, event | category | flops | bytes accessed | tf_op | source)
XLA Modules:
  0.0 31.4 jit_solution(1940226124238202958)
XLA Ops:
  0.6 30.0 %section.1 = (f32[8,4,16,128]{3,2,1,0:T(8,128)S(1)}, f32[3,4,16,128]{3,2,1,0:T(8,128)S(1)}) custom-call(f32[8,4,16,128]{3,2,1,0:T(8,128)} %cells_hbm.1, f32[3,4,16,128]{3,2,1,0:T(8,128)} %faces_hbm.1), custom_call_target="tpu_custom_call" | custom-call | tf_op jit(solution)/shard_map/section/pallas_call | solution.py:492
  30.6 0.7 %write_out.1 = (f32[8,4,16,128]{3,2,1,0:T(8,128)}, f32[3,4,16,128]{3,2,1,0:T(8,128)}) custom-call(f32[8,4,16,128]{3,2,1,0:T(8,128)S(1)} %get-tuple-element.4.state, f32[3,4,16,128]{3,2,1,0:T(8,128)S(1)} %get-tuple-element.5.faces_new), custom_call_target="tpu_custom_call" | custom-call | tf_op jit(solution)/shard_map/write_out/pallas_call | solution.py:526

commit v3 on v2

--- a/solution.py
+++ b/solution.py
@@ -12,7 +12,7 @@
 
 ROW_UP, ROW_DOWN, FACE_R, PACK_UP, PACK_DOWN, TH_UP, TH_DOWN, FACE_T = range(8)
 CORNER_UP, CORNER_DOWN, PAIR_UP, PAIR_DOWN, LOW_UP, LOW_DOWN, HIGH_UP, HIGH_DOWN = range(8, 16)
-DIRECT = 16
+E1_UP, E1_DOWN, DIRECT = 16, 17, 18
 
 
 def cell_state(w):
@@ -63,8 +63,8 @@
 
 def kernel(
     cells_hbm, faces_hbm, state, faces_new,
-    cv, fv, first_rows, rlo, rhi, f0hi, packs, gp, th_src, gt, f1_src, f1hi, cr_src, cr, pr, e1_own, e1_src, e1f,
-    load_sem, send_sem, recv_sem, ok_near, ok_wrap, ok_th,
+    cv, fv, first_rows, rlo, rhi, f0hi, packs, gp, th_src, gt, f1_src, f1hi, cr_src, cr, pr, e1_corner, e1_src, e1g, e1f,
+    load_sem, send_sem, recv_sem, ok_near, ok_wrap, ok_th, ok_side, ok_row,
 ):
     row = lax.axis_index("row")
     th = lax.axis_index("th")
@@ -75,7 +75,9 @@
     at_bottom, at_top = row == 0, row == rows - 1
     at_north, at_south = th == 0, th == ths - 1
     first_z = z == 0
-    corner_sender = (z == 2 * phs - 1) & (row > 0)
+    corner_place = z == 2 * phs - 1
+    beside_corner = z == 2 * phs - 2
+    corner_sender = corner_place & (row > 0)
 
     def place(dr=0, dt=0, dp=0):
         return {"row": row + dr, "th": th + dt, "ph": lax.rem(ph + dp + phs, phs)}
@@ -108,8 +110,11 @@
     has_up, has_down = th < ths - 1, th > 0
     first_p, last_p = ph == 0, ph == phs - 1
     inner_up, inner_down = ph < phs - 1, ph > 0
-    tell(barrier, row < rows - 1, place(dr=1))
-    tell(barrier, row > 0, place(dr=-1))
+    row_up, row_down = row < rows - 1, row > 0
+    plain = jnp.logical_not(corner_place)
+    tell(barrier, row_up & plain, place(dr=1))
+    tell(barrier, row_down & plain, place(dr=-1))
+    tell(barrier, corner_place, place(dp=-1))
     tell(barrier, inner_up, place(dp=1))
     tell(barrier, has_up, place(dt=1))
     tell(barrier, first_p, place(dp=-1))
@@ -139,12 +144,14 @@
         CORNER_DOWN: copy(CORNER_DOWN, cr_src.at[0], cr.at[1], down_t),
         PAIR_UP: copy(PAIR_UP, gp, pr.at[0], up_r),
         PAIR_DOWN: copy(PAIR_DOWN, gp, pr.at[1], down_r),
-        LOW_UP: copy(LOW_UP, e1_src.at[0], e1f.at[0, 0], up_p),
-        LOW_DOWN: copy(LOW_DOWN, e1_src.at[0], e1f.at[1, 0], down_p),
-        HIGH_UP: copy(HIGH_UP, e1_src.at[1], e1f.at[0, 1], up_p),
-        HIGH_DOWN: copy(HIGH_DOWN, e1_src.at[1], e1f.at[1, 1], down_p),
+        E1_UP: copy(E1_UP, e1_src.at[1], e1g.at[0], up_t),
+        E1_DOWN: copy(E1_DOWN, e1_src.at[0], e1g.at[1], down_t),
+        LOW_UP: copy(LOW_UP, e1g.at[0], e1f.at[0, 0], up_p),
+        LOW_DOWN: copy(LOW_DOWN, e1g.at[0], e1f.at[1, 0], down_p),
+        HIGH_UP: copy(HIGH_UP, e1g.at[1], e1f.at[0, 1], up_p),
+        HIGH_DOWN: copy(HIGH_DOWN, e1g.at[1], e1f.at[1, 1], down_p),
     }
-    direct_left = copy(DIRECT, e1_own, e1f.at[0, 1], origin, HIGH_UP)
+    direct_left = copy(DIRECT, e1_corner, e1f.at[0, 1], origin, HIGH_UP)
 
     def send(kind, condition=None):
         if condition is None:
@@ -164,7 +171,7 @@
         load_field.wait()
         for r in range(4):
             w = [first_rows[k, r, 0:1] for k in range(4)]
-            e1_own[r : r + 1] = -(w[0] * w[3] - w[1] * w[2])
+            e1_corner[r : r + 1] = -(w[0] * w[3] - w[1] * w[2])
 
     def number(*conditions):
         total = jnp.int32(0)
@@ -172,21 +179,29 @@
             total = total + condition.astype(jnp.int32)
         return total
 
-    pl.semaphore_wait(barrier, number(corner_sender, has_down, last_p, row > 0, row < rows - 1, inner_down))
+    pl.semaphore_wait(
+        barrier,
+        number(corner_sender, has_down, last_p, row_down & plain, row_up & plain, inner_down, beside_corner),
+    )
     pl.when(corner_sender)(direct_left.start)
     tell(ok_th, has_down, place(dt=-1))
     tell(ok_wrap, last_p, place(dp=1))
-    tell(ok_near, inner_down, place(dp=-1))
+    tell(ok_near, inner_down & plain, place(dp=-1))
+    tell(ok_side, beside_corner & row_up, place(dr=1))
+    tell(ok_side, beside_corner & row_down, place(dr=-1))
 
     load_cells.wait()
-    send(ROW_UP, row < rows - 1)
-    send(ROW_DOWN, row > 0)
+    send(ROW_UP, row_up & plain)
+    send(ROW_DOWN, row_down & plain)
     for r in range(4):
         for f in range(8):
             th_src[0, f * 4 + r : f * 4 + r + 1] = cv[f, r, 0:1]
             th_src[1, f * 4 + r : f * 4 + r + 1] = cv[f, r, 15:16]
+    for side in range(2):
+        e1_src[side] = emf([th_src[side, f * 4 : f * 4 + 4] for f in range(8)], 0)
+    send(E1_DOWN, has_down)
     load_faces.wait()
-    send(FACE_R, row > 0)
+    send(FACE_R, row_down & plain)
     for r in range(4):
         f1_src[r : r + 1] = fv[1, r, 0:1]
     third = fv[2].reshape(64, 128)
@@ -225,12 +240,26 @@
 
     @pl.when(at_north)
     def _():
-        e1_src[0] = emf(ghost_rows(0), 0)
+        e1g[0] = emf(ghost_rows(0), 0)
+
+    @pl.when(at_south)
+    def _():
+        e1g[1] = emf(ghost_rows(1), 0)
 
     send(PACK_DOWN, inner_down)
     send(PACK_UP, last_p)
     send(LOW_DOWN, at_north & inner_down)
     send(LOW_UP, at_north & last_p)
+
+    @pl.when(beside_corner)
+    def _():
+        pl.semaphore_wait(ok_side, number(row_up, row_down))
+
+    tell(ok_row, beside_corner, place(dp=1))
+    told(ok_row, corner_place)
+    send(ROW_UP, row_up & corner_place)
+    send(ROW_DOWN, row_down & corner_place)
+    send(FACE_R, row_down & corner_place)
 
     arrived(ROW_UP, row > 0)
     arrived(ROW_DOWN, row < rows - 1)
@@ -252,7 +281,7 @@
     fill_corner(1, 15, at_south)
     send(CORNER_DOWN, has_down)
 
-    told(ok_near, inner_up)
+    told(ok_near, inner_up & jnp.logical_not(beside_corner))
     send(PACK_UP, inner_up)
     send(LOW_UP, at_north & inner_up)
 
@@ -293,6 +322,7 @@
 
     def send_up(condition):
         told(ok_th, condition)
+        send(E1_UP, condition)
         send(TH_UP, condition)
         send(CORNER_UP, condition)
 
@@ -337,20 +367,17 @@
     apply(2, beside, ahead_p, behind_p, left, right)
     send_up(has_up & jnp.logical_not(last_p))
 
-    arrived(TH_UP, th > 0)
-
-    @pl.when(th > 0)
-    def _():
-        e1_src[0] = emf(ghost_rows(0), 0)
-
-    send(LOW_UP, th > 0)
-    send(LOW_DOWN, th > 0)
-    arrived(TH_DOWN, th < ths - 1)
-    arrived(FACE_T, th < ths - 1)
-    e1_src[1] = emf(ghost_rows(1), 0)
+    arrived(E1_UP, has_down)
+    send(LOW_UP, has_down)
+    send(LOW_DOWN, has_down)
+    arrived(E1_DOWN, has_up)
     high_up = (z != phs - 1) | (row == 0)
     send(HIGH_UP, high_up)
     send(HIGH_DOWN)
+
+    arrived(TH_UP, has_down)
+    arrived(TH_DOWN, has_up)
+    arrived(FACE_T, has_up)
 
     north, south = line == 0, line == 15
 
@@ -437,42 +464,53 @@
     faces_new[1] = new_second
     state[6] = 0.5 * (new_second + jnp.where(south, new_upper, ahead_t(new_second)))
 
-    arrived(LOW_UP)
-    arrived(LOW_DOWN)
-    arrived(HIGH_DOWN)
-    arrived(HIGH_UP)
-    lane4 = lax.broadcasted_iota(jnp.int32, (4, 128), 1)
-
-    def corner_rows(k):
-        a = jnp.where(lane4 == 0, pltpu.roll(e1f[0, k], 1, 1), 0.0)
-        b = jnp.where(lane4 == 127, pltpu.roll(e1f[1, k], 127, 1), 0.0)
-        return QUARTER * a, QUARTER * b
-
-    a_low, b_low = corner_rows(0)
-    a_high, b_high = corner_rows(1)
-    keep = jnp.where(at_south, 0.0, 0.5)
-    for r in range(4):
-        a, b = a_low[r : r + 1], b_low[r : r + 1]
-        faces_new[1, r, 0:1] = faces_new[1, r, 0:1] - (b - a)
-        state[6, r, 0:1] = state[6, r, 0:1] - 0.5 * (b - a)
-        faces_new[2, r, 0:1] = faces_new[2, r, 0:1] - a
-        state[7, r, 0:1] = state[7, r, 0:1] - 0.5 * (a + b)
-        a, b = a_high[r : r + 1], b_high[r : r + 1]
-        state[6, r, 15:16] = state[6, r, 15:16] - keep * (b - a)
-        faces_new[2, r, 15:16] = faces_new[2, r, 15:16] + a
-        state[7, r, 15:16] = state[7, r, 15:16] + 0.5 * (a + b)
-
     for kind, condition in (
-        (ROW_UP, row < rows - 1), (ROW_DOWN, row > 0), (FACE_R, row > 0), (PACK_UP, None), (PACK_DOWN, None),
-        (TH_UP, th < ths - 1), (TH_DOWN, th > 0), (FACE_T, th > 0), (CORNER_UP, th < ths - 1), (CORNER_DOWN, th > 0),
-        (PAIR_UP, row < rows - 1), (PAIR_DOWN, row > 0), (LOW_UP, None), (LOW_DOWN, None),
-        (HIGH_UP, high_up), (HIGH_DOWN, None),
+        (ROW_UP, row_up), (ROW_DOWN, row_down), (FACE_R, row_down), (PACK_UP, None), (PACK_DOWN, None),
+        (TH_UP, has_up), (TH_DOWN, has_down), (FACE_T, has_down), (CORNER_UP, has_up), (CORNER_DOWN, has_down),
+        (PAIR_UP, row_up), (PAIR_DOWN, row_down), (LOW_UP, None), (LOW_DOWN, None),
+        (HIGH_UP, high_up), (HIGH_DOWN, None), (E1_UP, has_up), (E1_DOWN, has_down),
     ):
         if condition is None:
             copies[kind].wait_send()
         else:
             pl.when(condition)(copies[kind].wait_send)
     pl.when(corner_sender)(direct_left.wait_send)
+
+    lane4 = lax.broadcasted_iota(jnp.int32, (4, 128), 1)
+
+    def from_left(k):
+        return QUARTER * jnp.where(lane4 == 0, pltpu.roll(e1f[0, k], 1, 1), 0.0)
+
+    def from_right(k):
+        return QUARTER * jnp.where(lane4 == 127, pltpu.roll(e1f[1, k], 127, 1), 0.0)
+
+    keep = jnp.where(at_south, 0.0, 0.5)
+
+    def adjust(ref, r, place_row, amount):
+        ref[r, place_row : place_row + 1] = ref[r, place_row : place_row + 1] + amount
+
+    arrived(LOW_UP)
+    arrived(LOW_DOWN)
+    a_low, b_low = from_left(0), from_right(0)
+    for r in range(4):
+        a, b = a_low[r : r + 1], b_low[r : r + 1]
+        adjust(faces_new.at[1], r, 0, a - b)
+        adjust(state.at[6], r, 0, 0.5 * (a - b))
+        adjust(faces_new.at[2], r, 0, -a)
+        adjust(state.at[7], r, 0, -0.5 * (a + b))
+    arrived(HIGH_DOWN)
+    b_high = from_right(1)
+    for r in range(4):
+        b = b_high[r : r + 1]
+        adjust(state.at[6], r, 15, -keep * b)
+        adjust(state.at[7], r, 15, 0.5 * b)
+    arrived(HIGH_UP)
+    a_high = from_left(1)
+    for r in range(4):
+        a = a_high[r : r + 1]
+        adjust(state.at[6], r, 15, keep * a)
+        adjust(faces_new.at[2], r, 15, a)
+        adjust(state.at[7], r, 15, 0.5 * a)
 
 
 def write_out(state, faces_new, state_hbm, faces_hbm, sem):
@@ -512,10 +550,13 @@
             pltpu.VMEM((2, 2, 8, 128), f32),
             pltpu.VMEM((4, 128), f32),
             pltpu.VMEM((2, 4, 128), f32),
+            pltpu.VMEM((2, 4, 128), f32),
             pltpu.VMEM((2, 2, 4, 128), f32),
             pltpu.SemaphoreType.DMA((4,)),
-            pltpu.SemaphoreType.DMA((17,)),
-            pltpu.SemaphoreType.DMA((17,)),
+            pltpu.SemaphoreType.DMA((19,)),
+            pltpu.SemaphoreType.DMA((19,)),
+            pltpu.SemaphoreType.REGULAR,
+            pltpu.SemaphoreType.REGULAR,
             pltpu.SemaphoreType.REGULAR,
             pltpu.SemaphoreType.REGULAR,
             pltpu.SemaphoreType.REGULAR,

time: 31.5 us -> 29.7 us (0.943)
  Pallas kernels: 30.7 us -> 28.8 us
    pallas_call x1, Pallas kernels: 30 us -> 28.1 us  [on_device(): pl.pallas_call(kernel, out_shape=tuple((pltpu.VMEM(shape, f32) for shape...]
where the time goes in v3:
time: 29.7 us; the launch traced here: 29.5 us
  Pallas kernels  28.8 us (97%)
  between operations  0.64 us (2%)
    pallas_call x1, Pallas kernels, on_device(): pl.pallas_call(kernel, out_shape=tuple((pltpu.VMEM(shape, f32) for shape...  28.1 us
    pallas_call x1, Pallas kernels, on_device(): pl.pallas_call(write_out, out_shape=tuple((jax.ShapeDtypeStruct(shape, f3...  0.75 us

profile of v3, /device:TPU:6, one launch (start us, length us, event | category | flops | bytes accessed | tf_op | source)
XLA Modules:
  0.0 29.5 jit_solution(1954936219882710692)
XLA Ops:
  0.6 28.1 %section.1 = (f32[8,4,16,128]{3,2,1,0:T(8,128)S(1)}, f32[3,4,16,128]{3,2,1,0:T(8,128)S(1)}) custom-call(f32[8,4,16,128]{3,2,1,0:T(8,128)} %cells_hbm.1, f32[3,4,16,128]{3,2,1,0:T(8,128)} %faces_hbm.1), custom_call_target="tpu_custom_call" | custom-call | tf_op jit(solution)/shard_map/section/pallas_call | solution.py:530
  28.7 0.7 %write_out.1 = (f32[8,4,16,128]{3,2,1,0:T(8,128)}, f32[3,4,16,128]{3,2,1,0:T(8,128)}) custom-call(f32[8,4,16,128]{3,2,1,0:T(8,128)S(1)} %get-tuple-element.4.state, f32[3,4,16,128]{3,2,1,0:T(8,128)S(1)} %get-tuple-element.5.faces_new), custom_call_target="tpu_custom_call" | custom-call | tf_op jit(solution)/shard_map/write_out/pallas_call | solution.py:567

commit v4 on v3

--- a/solution.py
+++ b/solution.py
@@ -13,6 +13,33 @@
 ROW_UP, ROW_DOWN, FACE_R, PACK_UP, PACK_DOWN, TH_UP, TH_DOWN, FACE_T = range(8)
 CORNER_UP, CORNER_DOWN, PAIR_UP, PAIR_DOWN, LOW_UP, LOW_DOWN, HIGH_UP, HIGH_DOWN = range(8, 16)
 E1_UP, E1_DOWN, DIRECT = 16, 17, 18
+
+LEAVE = (
+    ((ROW_UP, PAIR_UP), 144),
+    ((ROW_DOWN, FACE_R, PAIR_DOWN), 160),
+    ((TH_UP, CORNER_UP, E1_UP), 38),
+    ((TH_DOWN, FACE_T, CORNER_DOWN, E1_DOWN), 42),
+    ((PACK_UP, PACK_DOWN, LOW_UP, LOW_DOWN, HIGH_DOWN), 28),
+    ((HIGH_UP,), 4),
+    ((DIRECT,), 4),
+)
+ARRIVE = (
+    ((ROW_UP,), 128),
+    ((ROW_DOWN, FACE_R), 144),
+    ((PACK_UP, PACK_DOWN), 16),
+    ((TH_UP, CORNER_UP), 34),
+    ((TH_DOWN, FACE_T, CORNER_DOWN), 38),
+    ((PAIR_UP,), 16),
+    ((PAIR_DOWN,), 16),
+    ((LOW_UP, HIGH_UP), 8),
+    ((LOW_DOWN, HIGH_DOWN), 8),
+    ((E1_UP,), 4),
+    ((E1_DOWN,), 4),
+)
+
+
+def group_of(groups, kind):
+    return next(i for i, (kinds, _) in enumerate(groups) if kind in kinds)
 
 
 def cell_state(w):
@@ -63,8 +90,8 @@
 
 def kernel(
     cells_hbm, faces_hbm, state, faces_new,
-    cv, fv, first_rows, rlo, rhi, f0hi, packs, gp, th_src, gt, f1_src, f1hi, cr_src, cr, pr, e1_corner, e1_src, e1g, e1f,
-    load_sem, send_sem, recv_sem, ok_near, ok_wrap, ok_th, ok_side, ok_row,
+    cv, fv, first_rows, rlo, rhi, f0hi, packs, gp, th_src, gt, f1_src, f1hi, cr_src, cr, pr, e1_corner, e1_src, e1g, e1f, tokens,
+    load_sem, send_sem, recv_sem, ok_near, ok_wrap, ok_th,
 ):
     row = lax.axis_index("row")
     th = lax.axis_index("th")
@@ -77,7 +104,7 @@
     first_z = z == 0
     corner_place = z == 2 * phs - 1
     beside_corner = z == 2 * phs - 2
-    corner_sender = corner_place & (row > 0)
+    corner_sender = (corner_place & (row > 0)) | ((z == phs) & (row == 0))
 
     def place(dr=0, dt=0, dp=0):
         return {"row": row + dr, "th": th + dt, "ph": lax.rem(ph + dp + phs, phs)}
@@ -85,7 +112,7 @@
     load_cells = pltpu.make_async_copy(cells_hbm, cv, load_sem.at[0])
     load_faces = pltpu.make_async_copy(faces_hbm, fv, load_sem.at[1])
     load_velocity = pltpu.make_async_copy(cells_hbm.at[2:4, :, 0:8], first_rows.at[0:2], load_sem.at[2])
-    load_field = pltpu.make_async_copy(cells_hbm.at[6:8, :, 0:8], first_rows.at[2:4], load_sem.at[3])
+    load_field = pltpu.make_async_copy(cells_hbm.at[6:8, :, 0:8], first_rows.at[2:4], load_sem.at[2])
 
     @pl.when(corner_sender)
     def _():
@@ -119,18 +146,19 @@
     tell(barrier, has_up, place(dt=1))
     tell(barrier, first_p, place(dp=-1))
     tell(barrier, (z == 0) & (row > 0), {"row": row, "th": 1, "ph": phs - 1})
+    tell(barrier, (z == 1) & (row == 0), {"row": row, "th": 1, "ph": 0})
 
     def copy(kind, src, dst, target, recv=None):
         return pltpu.make_async_remote_copy(
-            src_ref=src, dst_ref=dst, send_sem=send_sem.at[kind],
-            recv_sem=recv_sem.at[kind if recv is None else recv],
+            src_ref=src, dst_ref=dst, send_sem=send_sem.at[group_of(LEAVE, kind)],
+            recv_sem=recv_sem.at[group_of(ARRIVE, kind if recv is None else recv)],
             device_id=target, device_id_type=MESH,
         )
 
     up_r, down_r = place(dr=1), place(dr=-1)
     up_t, down_t = place(dt=1), place(dt=-1)
     up_p, down_p = place(dp=1), place(dp=-1)
-    origin = {"row": row, "th": th * 0, "ph": ph * 0}
+    origin = {"row": row, "th": th * 0, "ph": (row == 0).astype(jnp.int32)}
     copies = {
         ROW_UP: copy(ROW_UP, cv.at[:, 3], rlo, up_r),
         ROW_DOWN: copy(ROW_DOWN, cv.at[:, 0], rhi, down_r),
@@ -159,16 +187,24 @@
         else:
             pl.when(condition)(copies[kind].start)
 
+    def all_of(groups, semaphores, kind, condition):
+        group = group_of(groups, kind)
+        part = tokens.at[0 : groups[group][1]]
+        wait = pltpu.make_async_copy(part, part, semaphores.at[group]).wait
+        if condition is None:
+            wait()
+        else:
+            pl.when(condition)(wait)
+
     def arrived(kind, condition=None):
-        if condition is None:
-            copies[kind].wait_recv()
-        else:
-            pl.when(condition)(copies[kind].wait_recv)
+        all_of(ARRIVE, recv_sem, kind, condition)
+
+    def left_here(kind, condition=None):
+        all_of(LEAVE, send_sem, kind, condition)
 
     @pl.when(corner_sender)
     def _():
-        load_velocity.wait()
-        load_field.wait()
+        pltpu.make_async_copy(first_rows, first_rows, load_sem.at[2]).wait()
         for r in range(4):
             w = [first_rows[k, r, 0:1] for k in range(4)]
             e1_corner[r : r + 1] = -(w[0] * w[3] - w[1] * w[2])
@@ -187,8 +223,8 @@
     tell(ok_th, has_down, place(dt=-1))
     tell(ok_wrap, last_p, place(dp=1))
     tell(ok_near, inner_down & plain, place(dp=-1))
-    tell(ok_side, beside_corner & row_up, place(dr=1))
-    tell(ok_side, beside_corner & row_down, place(dr=-1))
+    tell(ok_near, beside_corner & row_up, place(dr=1))
+    tell(ok_near, beside_corner & row_down, place(dr=-1))
 
     load_cells.wait()
     send(ROW_UP, row_up & plain)
@@ -253,17 +289,16 @@
 
     @pl.when(beside_corner)
     def _():
-        pl.semaphore_wait(ok_side, number(row_up, row_down))
-
-    tell(ok_row, beside_corner, place(dp=1))
-    told(ok_row, corner_place)
+        pl.semaphore_wait(ok_near, number(row_up, row_down))
+
+    tell(ok_near, beside_corner, place(dp=1))
+    told(ok_near, corner_place)
     send(ROW_UP, row_up & corner_place)
     send(ROW_DOWN, row_down & corner_place)
     send(FACE_R, row_down & corner_place)
 
-    arrived(ROW_UP, row > 0)
-    arrived(ROW_DOWN, row < rows - 1)
-    arrived(FACE_R, row < rows - 1)
+    arrived(ROW_UP, row_down)
+    arrived(ROW_DOWN, row_up)
     for side, line in ((0, 0), (1, 15)):
         for k, ghost in enumerate((rlo, rhi)):
             w = [ghost[f, line : line + 1] for f in range(8)]
@@ -323,15 +358,12 @@
     def send_up(condition):
         told(ok_th, condition)
         send(E1_UP, condition)
-        send(TH_UP, condition)
-        send(CORNER_UP, condition)
 
     send_up(has_up & last_p)
 
-    arrived(PACK_DOWN)
     arrived(PACK_UP)
-    send(PAIR_UP, row < rows - 1)
-    send(PAIR_DOWN, row > 0)
+    send(PAIR_UP, row_up)
+    send(PAIR_DOWN, row_down)
     columns = jnp.concatenate([gp[0], gp[1]], axis=0).T
 
     def column(side, c, half):
@@ -371,13 +403,14 @@
     send(LOW_UP, has_down)
     send(LOW_DOWN, has_down)
     arrived(E1_DOWN, has_up)
-    high_up = (z != phs - 1) | (row == 0)
+    high_up = jnp.logical_not(((z == phs - 1) & (row > 0)) | ((z == 0) & (row == 0)))
     send(HIGH_UP, high_up)
     send(HIGH_DOWN)
+    send(TH_UP, has_up)
+    send(CORNER_UP, has_up)
 
     arrived(TH_UP, has_down)
     arrived(TH_DOWN, has_up)
-    arrived(FACE_T, has_up)
 
     north, south = line == 0, line == 15
 
@@ -392,10 +425,8 @@
     apply(1, outside, ahead_t, behind_t, north, south)
     e1_outside, e3_outside = emf(outside, 0), emf(outside, 2)
 
-    arrived(CORNER_UP, th > 0)
-    arrived(CORNER_DOWN, th < ths - 1)
-    arrived(PAIR_UP, row > 0)
-    arrived(PAIR_DOWN, row < rows - 1)
+    arrived(PAIR_UP, row_down)
+    arrived(PAIR_DOWN, row_up)
 
     def pair_emf(ref, *index):
         rows8 = ref[index] if index else ref[...]
@@ -464,17 +495,13 @@
     faces_new[1] = new_second
     state[6] = 0.5 * (new_second + jnp.where(south, new_upper, ahead_t(new_second)))
 
-    for kind, condition in (
-        (ROW_UP, row_up), (ROW_DOWN, row_down), (FACE_R, row_down), (PACK_UP, None), (PACK_DOWN, None),
-        (TH_UP, has_up), (TH_DOWN, has_down), (FACE_T, has_down), (CORNER_UP, has_up), (CORNER_DOWN, has_down),
-        (PAIR_UP, row_up), (PAIR_DOWN, row_down), (LOW_UP, None), (LOW_DOWN, None),
-        (HIGH_UP, high_up), (HIGH_DOWN, None), (E1_UP, has_up), (E1_DOWN, has_down),
-    ):
-        if condition is None:
-            copies[kind].wait_send()
-        else:
-            pl.when(condition)(copies[kind].wait_send)
-    pl.when(corner_sender)(direct_left.wait_send)
+    left_here(ROW_UP, row_up)
+    left_here(ROW_DOWN, row_down)
+    left_here(TH_UP, has_up)
+    left_here(TH_DOWN, has_down)
+    left_here(PACK_UP)
+    left_here(HIGH_UP, high_up)
+    left_here(DIRECT, corner_sender)
 
     lane4 = lax.broadcasted_iota(jnp.int32, (4, 128), 1)
 
@@ -489,24 +516,24 @@
     def adjust(ref, r, place_row, amount):
         ref[r, place_row : place_row + 1] = ref[r, place_row : place_row + 1] + amount
 
-    arrived(LOW_UP)
     arrived(LOW_DOWN)
-    a_low, b_low = from_left(0), from_right(0)
+    b_low, b_high = from_right(0), from_right(1)
     for r in range(4):
-        a, b = a_low[r : r + 1], b_low[r : r + 1]
-        adjust(faces_new.at[1], r, 0, a - b)
-        adjust(state.at[6], r, 0, 0.5 * (a - b))
-        adjust(faces_new.at[2], r, 0, -a)
-        adjust(state.at[7], r, 0, -0.5 * (a + b))
-    arrived(HIGH_DOWN)
-    b_high = from_right(1)
-    for r in range(4):
+        b = b_low[r : r + 1]
+        adjust(faces_new.at[1], r, 0, -b)
+        adjust(state.at[6], r, 0, -0.5 * b)
+        adjust(state.at[7], r, 0, -0.5 * b)
         b = b_high[r : r + 1]
         adjust(state.at[6], r, 15, -keep * b)
         adjust(state.at[7], r, 15, 0.5 * b)
-    arrived(HIGH_UP)
-    a_high = from_left(1)
+    arrived(LOW_UP)
+    a_low, a_high = from_left(0), from_left(1)
     for r in range(4):
+        a = a_low[r : r + 1]
+        adjust(faces_new.at[1], r, 0, a)
+        adjust(state.at[6], r, 0, 0.5 * a)
+        adjust(faces_new.at[2], r, 0, -a)
+        adjust(state.at[7], r, 0, -0.5 * a)
         a = a_high[r : r + 1]
         adjust(state.at[6], r, 15, keep * a)
         adjust(faces_new.at[2], r, 15, a)
@@ -552,11 +579,10 @@
             pltpu.VMEM((2, 4, 128), f32),
             pltpu.VMEM((2, 4, 128), f32),
             pltpu.VMEM((2, 2, 4, 128), f32),
-            pltpu.SemaphoreType.DMA((4,)),
-            pltpu.SemaphoreType.DMA((19,)),
-            pltpu.SemaphoreType.DMA((19,)),
-            pltpu.SemaphoreType.REGULAR,
-            pltpu.SemaphoreType.REGULAR,
+            pltpu.VMEM((160, 1, 128), f32),
+            pltpu.SemaphoreType.DMA((3,)),
+            pltpu.SemaphoreType.DMA((len(LEAVE),)),
+            pltpu.SemaphoreType.DMA((len(ARRIVE),)),
             pltpu.SemaphoreType.REGULAR,
             pltpu.SemaphoreType.REGULAR,
             pltpu.SemaphoreType.REGULAR,

time: 29.7 us -> 29.6 us (level)
  no operation moved by 1% of the time
where the time goes in v4:
time: 29.6 us; the launch traced here: 29.3 us
  Pallas kernels  28.6 us (97%)
  between operations  0.64 us (2%)
    pallas_call x1, Pallas kernels, on_device(): pl.pallas_call(kernel, out_shape=tuple((pltpu.VMEM(shape, f32) for shape...  27.9 us
    pallas_call x1, Pallas kernels, on_device(): pl.pallas_call(write_out, out_shape=tuple((jax.ShapeDtypeStruct(shape, f3...  0.75 us

profile of v4, /device:TPU:6, one launch (start us, length us, event | category | flops | bytes accessed | tf_op | source)
XLA Modules:
  0.0 29.3 jit_solution(11938999706400631616)
XLA Ops:
  0.6 27.9 %section.1 = (f32[8,4,16,128]{3,2,1,0:T(8,128)S(1)}, f32[3,4,16,128]{3,2,1,0:T(8,128)S(1)}) custom-call(f32[8,4,16,128]{3,2,1,0:T(8,128)} %cells_hbm.1, f32[3,4,16,128]{3,2,1,0:T(8,128)} %faces_hbm.1), custom_call_target="tpu_custom_call" | custom-call | tf_op jit(solution)/shard_map/section/pallas_call | solution.py:557
  28.5 0.7 %write_out.1 = (f32[8,4,16,128]{3,2,1,0:T(8,128)}, f32[3,4,16,128]{3,2,1,0:T(8,128)}) custom-call(f32[8,4,16,128]{3,2,1,0:T(8,128)S(1)} %get-tuple-element.4.state, f32[3,4,16,128]{3,2,1,0:T(8,128)S(1)} %get-tuple-element.5.faces_new), custom_call_target="tpu_custom_call" | custom-call | tf_op jit(solution)/shard_map/write_out/pallas_call | solution.py:593

commit v5 on v4

--- a/solution.py
+++ b/solution.py
@@ -14,32 +14,27 @@
 CORNER_UP, CORNER_DOWN, PAIR_UP, PAIR_DOWN, LOW_UP, LOW_DOWN, HIGH_UP, HIGH_DOWN = range(8, 16)
 E1_UP, E1_DOWN, DIRECT = 16, 17, 18
 
+EDGE = 19
+
 LEAVE = (
-    ((ROW_UP, PAIR_UP), 144),
-    ((ROW_DOWN, FACE_R, PAIR_DOWN), 160),
-    ((TH_UP, CORNER_UP, E1_UP), 38),
-    ((TH_DOWN, FACE_T, CORNER_DOWN, E1_DOWN), 42),
-    ((PACK_UP, PACK_DOWN, LOW_UP, LOW_DOWN, HIGH_DOWN), 28),
-    ((HIGH_UP,), 4),
-    ((DIRECT,), 4),
+    (ROW_UP, PAIR_UP, ROW_DOWN, FACE_R, PAIR_DOWN),
+    (TH_UP, CORNER_UP, E1_UP, TH_DOWN, FACE_T, CORNER_DOWN, E1_DOWN),
+    (PACK_UP, PACK_DOWN, LOW_UP, LOW_DOWN, HIGH_UP, HIGH_DOWN, DIRECT, EDGE),
 )
 ARRIVE = (
-    ((ROW_UP,), 128),
-    ((ROW_DOWN, FACE_R), 144),
-    ((PACK_UP, PACK_DOWN), 16),
-    ((TH_UP, CORNER_UP), 34),
-    ((TH_DOWN, FACE_T, CORNER_DOWN), 38),
-    ((PAIR_UP,), 16),
-    ((PAIR_DOWN,), 16),
-    ((LOW_UP, HIGH_UP), 8),
-    ((LOW_DOWN, HIGH_DOWN), 8),
-    ((E1_UP,), 4),
-    ((E1_DOWN,), 4),
+    (ROW_UP, ROW_DOWN, FACE_R),
+    (PACK_UP, PACK_DOWN),
+    (TH_UP, CORNER_UP, TH_DOWN, FACE_T, CORNER_DOWN),
+    (PAIR_UP, PAIR_DOWN),
+    (LOW_UP, HIGH_UP),
+    (LOW_DOWN, HIGH_DOWN),
+    (E1_UP,),
+    (E1_DOWN,),
 )
 
 
 def group_of(groups, kind):
-    return next(i for i, (kinds, _) in enumerate(groups) if kind in kinds)
+    return next(i for i, kinds in enumerate(groups) if kind in kinds)
 
 
 def cell_state(w):
@@ -110,9 +105,9 @@
         return {"row": row + dr, "th": th + dt, "ph": lax.rem(ph + dp + phs, phs)}
 
     load_cells = pltpu.make_async_copy(cells_hbm, cv, load_sem.at[0])
-    load_faces = pltpu.make_async_copy(faces_hbm, fv, load_sem.at[1])
-    load_velocity = pltpu.make_async_copy(cells_hbm.at[2:4, :, 0:8], first_rows.at[0:2], load_sem.at[2])
-    load_field = pltpu.make_async_copy(cells_hbm.at[6:8, :, 0:8], first_rows.at[2:4], load_sem.at[2])
+    load_faces = pltpu.make_async_copy(faces_hbm, fv, load_sem.at[0])
+    load_velocity = pltpu.make_async_copy(cells_hbm.at[2:4, :, 0:8], first_rows.at[0:2], load_sem.at[1])
+    load_field = pltpu.make_async_copy(cells_hbm.at[6:8, :, 0:8], first_rows.at[2:4], load_sem.at[1])
 
     @pl.when(corner_sender)
     def _():
@@ -142,6 +137,13 @@
     tell(barrier, row_up & plain, place(dr=1))
     tell(barrier, row_down & plain, place(dr=-1))
     tell(barrier, corner_place, place(dp=-1))
+    edge = last_p & has_up
+    before_edge = first_p & has_down
+    twin_below = (th == ths - 2) & inner_up
+    twin_above = at_south & inner_up
+    past_edge = {"row": row, "th": th + 1, "ph": ph * 0}
+    tell(barrier, twin_above, place(dt=-1))
+    tell(barrier, edge, past_edge)
     tell(barrier, inner_up, place(dp=1))
     tell(barrier, has_up, place(dt=1))
     tell(barrier, first_p, place(dp=-1))
@@ -179,6 +181,7 @@
         HIGH_UP: copy(HIGH_UP, e1g.at[1], e1f.at[0, 1], up_p),
         HIGH_DOWN: copy(HIGH_DOWN, e1g.at[1], e1f.at[1, 1], down_p),
     }
+    edge_up = copy(EDGE, e1_src.at[1], e1f.at[0, 0], past_edge, LOW_UP)
     direct_left = copy(DIRECT, e1_corner, e1f.at[0, 1], origin, HIGH_UP)
 
     def send(kind, condition=None):
@@ -187,24 +190,28 @@
         else:
             pl.when(condition)(copies[kind].start)
 
-    def all_of(groups, semaphores, kind, condition):
-        group = group_of(groups, kind)
-        part = tokens.at[0 : groups[group][1]]
-        wait = pltpu.make_async_copy(part, part, semaphores.at[group]).wait
+    def take(semaphore, size, condition=None):
+        part = tokens.at[0:size]
+        wait = pltpu.make_async_copy(part, part, semaphore).wait
         if condition is None:
             wait()
         else:
             pl.when(condition)(wait)
 
-    def arrived(kind, condition=None):
-        all_of(ARRIVE, recv_sem, kind, condition)
-
-    def left_here(kind, condition=None):
-        all_of(LEAVE, send_sem, kind, condition)
+    def take_sides(semaphore, first, first_size, second, second_size):
+        take(semaphore, first_size + second_size, first & second)
+        take(semaphore, first_size, first & jnp.logical_not(second))
+        take(semaphore, second_size, second & jnp.logical_not(first))
+
+    def arrived(kind):
+        return recv_sem.at[group_of(ARRIVE, kind)]
+
+    def leaving(kind):
+        return send_sem.at[group_of(LEAVE, kind)]
 
     @pl.when(corner_sender)
     def _():
-        pltpu.make_async_copy(first_rows, first_rows, load_sem.at[2]).wait()
+        pltpu.make_async_copy(first_rows, first_rows, load_sem.at[1]).wait()
         for r in range(4):
             w = [first_rows[k, r, 0:1] for k in range(4)]
             e1_corner[r : r + 1] = -(w[0] * w[3] - w[1] * w[2])
@@ -217,16 +224,18 @@
 
     pl.semaphore_wait(
         barrier,
-        number(corner_sender, has_down, last_p, row_down & plain, row_up & plain, inner_down, beside_corner),
+        number(corner_sender, has_down, last_p, row_down & plain, row_up & plain, inner_down, beside_corner)
+        + number(before_edge, twin_below),
     )
     pl.when(corner_sender)(direct_left.start)
-    tell(ok_th, has_down, place(dt=-1))
+    tell(ok_th, has_down & jnp.logical_not(twin_above), place(dt=-1))
+    tell(ok_wrap, before_edge, {"row": row, "th": th - 1, "ph": ph * 0 + phs - 1})
     tell(ok_wrap, last_p, place(dp=1))
     tell(ok_near, inner_down & plain, place(dp=-1))
     tell(ok_near, beside_corner & row_up, place(dr=1))
     tell(ok_near, beside_corner & row_down, place(dr=-1))
 
-    load_cells.wait()
+    take(load_sem.at[0], 704)
     send(ROW_UP, row_up & plain)
     send(ROW_DOWN, row_down & plain)
     for r in range(4):
@@ -236,7 +245,7 @@
     for side in range(2):
         e1_src[side] = emf([th_src[side, f * 4 : f * 4 + 4] for f in range(8)], 0)
     send(E1_DOWN, has_down)
-    load_faces.wait()
+    send(E1_UP, twin_below)
     send(FACE_R, row_down & plain)
     for r in range(4):
         f1_src[r : r + 1] = fv[1, r, 0:1]
@@ -247,6 +256,7 @@
         packs[1, c : c + 1] = turned[127:128]
     send(TH_DOWN, has_down)
     send(FACE_T, has_down)
+    send(TH_UP, twin_below)
     for c in range(4):
         turned = cv[2 * c : 2 * c + 2].reshape(128, 128).T
         packs[0, c : c + 1] = turned[0:1]
@@ -297,8 +307,7 @@
     send(ROW_DOWN, row_down & corner_place)
     send(FACE_R, row_down & corner_place)
 
-    arrived(ROW_UP, row_down)
-    arrived(ROW_DOWN, row_up)
+    take_sides(arrived(ROW_UP), row_down, 128, row_up, 144)
     for side, line in ((0, 0), (1, 15)):
         for k, ghost in enumerate((rlo, rhi)):
             w = [ghost[f, line : line + 1] for f in range(8)]
@@ -315,6 +324,7 @@
     fill_corner(0, 0, at_north)
     fill_corner(1, 15, at_south)
     send(CORNER_DOWN, has_down)
+    send(CORNER_UP, twin_below)
 
     told(ok_near, inner_up & jnp.logical_not(beside_corner))
     send(PACK_UP, inner_up)
@@ -351,17 +361,20 @@
     for i in range(5):
         state[i] = mid[0][i] - STEP * (face[i][1:] - face[i][:-1])
 
-    told(ok_wrap, first_p)
+    told(ok_wrap, first_p | edge)
+    pl.when(edge)(edge_up.start)
     send(PACK_DOWN, first_p)
     send(LOW_DOWN, at_north & first_p)
 
     def send_up(condition):
         told(ok_th, condition)
         send(E1_UP, condition)
+        send(TH_UP, condition)
+        send(CORNER_UP, condition)
 
     send_up(has_up & last_p)
 
-    arrived(PACK_UP)
+    take(arrived(PACK_UP), 16)
     send(PAIR_UP, row_up)
     send(PAIR_DOWN, row_down)
     columns = jnp.concatenate([gp[0], gp[1]], axis=0).T
@@ -397,20 +410,22 @@
             state[i] = state[i] - STEP * (upper[i] - below)
 
     apply(2, beside, ahead_p, behind_p, left, right)
-    send_up(has_up & jnp.logical_not(last_p))
-
-    arrived(E1_UP, has_down)
-    send(LOW_UP, has_down)
+    send_up(has_up & inner_up & jnp.logical_not(twin_below))
+
+    high_up = jnp.logical_not(((z == phs - 1) & (row > 0)) | ((z == 0) & (row == 0)))
+
+    def pass_high(condition):
+        take(arrived(E1_DOWN), 4, has_up & condition)
+        send(HIGH_UP, high_up & condition)
+        send(HIGH_DOWN, condition)
+
+    pass_high(last_p)
+    take(arrived(E1_UP), 4, has_down)
+    send(LOW_UP, has_down & inner_up)
     send(LOW_DOWN, has_down)
-    arrived(E1_DOWN, has_up)
-    high_up = jnp.logical_not(((z == phs - 1) & (row > 0)) | ((z == 0) & (row == 0)))
-    send(HIGH_UP, high_up)
-    send(HIGH_DOWN)
-    send(TH_UP, has_up)
-    send(CORNER_UP, has_up)
-
-    arrived(TH_UP, has_down)
-    arrived(TH_DOWN, has_up)
+    pass_high(inner_up)
+
+    take_sides(arrived(TH_UP), has_down, 34, has_up, 38)
 
     north, south = line == 0, line == 15
 
@@ -425,8 +440,7 @@
     apply(1, outside, ahead_t, behind_t, north, south)
     e1_outside, e3_outside = emf(outside, 0), emf(outside, 2)
 
-    arrived(PAIR_UP, row_down)
-    arrived(PAIR_DOWN, row_up)
+    take_sides(arrived(PAIR_UP), row_down, 16, row_up, 16)
 
     def pair_emf(ref, *index):
         rows8 = ref[index] if index else ref[...]
@@ -495,13 +509,11 @@
     faces_new[1] = new_second
     state[6] = 0.5 * (new_second + jnp.where(south, new_upper, ahead_t(new_second)))
 
-    left_here(ROW_UP, row_up)
-    left_here(ROW_DOWN, row_down)
-    left_here(TH_UP, has_up)
-    left_here(TH_DOWN, has_down)
-    left_here(PACK_UP)
-    left_here(HIGH_UP, high_up)
-    left_here(DIRECT, corner_sender)
+    take_sides(leaving(ROW_UP), row_up, 144, row_down, 160)
+    take_sides(leaving(TH_UP), has_up, 38, has_down, 42)
+    extra = number(inner_up | at_north, high_up, corner_sender, edge)
+    for k in range(5):
+        take(leaving(PACK_UP), 24 + 4 * k, extra == k)
 
     lane4 = lax.broadcasted_iota(jnp.int32, (4, 128), 1)
 
@@ -516,7 +528,7 @@
     def adjust(ref, r, place_row, amount):
         ref[r, place_row : place_row + 1] = ref[r, place_row : place_row + 1] + amount
 
-    arrived(LOW_DOWN)
+    take(arrived(LOW_DOWN), 8)
     b_low, b_high = from_right(0), from_right(1)
     for r in range(4):
         b = b_low[r : r + 1]
@@ -526,7 +538,7 @@
         b = b_high[r : r + 1]
         adjust(state.at[6], r, 15, -keep * b)
         adjust(state.at[7], r, 15, 0.5 * b)
-    arrived(LOW_UP)
+    take(arrived(LOW_UP), 8)
     a_low, a_high = from_left(0), from_left(1)
     for r in range(4):
         a = a_low[r : r + 1]
@@ -579,8 +591,8 @@
             pltpu.VMEM((2, 4, 128), f32),
             pltpu.VMEM((2, 4, 128), f32),
             pltpu.VMEM((2, 2, 4, 128), f32),
-            pltpu.VMEM((160, 1, 128), f32),
-            pltpu.SemaphoreType.DMA((3,)),
+            pltpu.VMEM((704, 1, 128), f32),
+            pltpu.SemaphoreType.DMA((2,)),
             pltpu.SemaphoreType.DMA((len(LEAVE),)),
             pltpu.SemaphoreType.DMA((len(ARRIVE),)),
             pltpu.SemaphoreType.REGULAR,

time: 29.6 us -> 29.6 us (level)
  no operation moved by 1% of the time
where the time goes in v5:
time: 29.6 us; the launch traced here: 29.2 us
  Pallas kernels  28.5 us (96%)
  between operations  0.64 us (2%)
    pallas_call x1, Pallas kernels, on_device(): pl.pallas_call(kernel, out_shape=tuple((pltpu.VMEM(shape, f32) for shape...  27.8 us
    pallas_call x1, Pallas kernels, on_device(): pl.pallas_call(write_out, out_shape=tuple((jax.ShapeDtypeStruct(shape, f3...  0.75 us

profile of v5, /device:TPU:6, one launch (start us, length us, event | category | flops | bytes accessed | tf_op | source)
XLA Modules:
  0.0 29.2 jit_solution(11426351666498058399)
XLA Ops:
  0.6 27.8 %section.1 = (f32[8,4,16,128]{3,2,1,0:T(8,128)S(1)}, f32[3,4,16,128]{3,2,1,0:T(8,128)S(1)}) custom-call(f32[8,4,16,128]{3,2,1,0:T(8,128)} %cells_hbm.1, f32[3,4,16,128]{3,2,1,0:T(8,128)} %faces_hbm.1), custom_call_target="tpu_custom_call" | custom-call | tf_op jit(solution)/shard_map/section/pallas_call | solution.py:569
  28.4 0.7 %write_out.1 = (f32[8,4,16,128]{3,2,1,0:T(8,128)}, f32[3,4,16,128]{3,2,1,0:T(8,128)}) custom-call(f32[8,4,16,128]{3,2,1,0:T(8,128)S(1)} %get-tuple-element.4.state, f32[3,4,16,128]{3,2,1,0:T(8,128)S(1)} %get-tuple-element.5.faces_new), custom_call_target="tpu_custom_call" | custom-call | tf_op jit(solution)/shard_map/write_out/pallas_call | solution.py:605

commit v6 on v5

--- a/solution.py
+++ b/solution.py
@@ -150,9 +150,12 @@
     tell(barrier, (z == 0) & (row > 0), {"row": row, "th": 1, "ph": phs - 1})
     tell(barrier, (z == 1) & (row == 0), {"row": row, "th": 1, "ph": 0})
 
+    def leaving(kind):
+        return (load_sem.at[0], send_sem, load_sem.at[1])[group_of(LEAVE, kind)]
+
     def copy(kind, src, dst, target, recv=None):
         return pltpu.make_async_remote_copy(
-            src_ref=src, dst_ref=dst, send_sem=send_sem.at[group_of(LEAVE, kind)],
+            src_ref=src, dst_ref=dst, send_sem=leaving(kind),
             recv_sem=recv_sem.at[group_of(ARRIVE, kind if recv is None else recv)],
             device_id=target, device_id_type=MESH,
         )
@@ -206,9 +209,6 @@
     def arrived(kind):
         return recv_sem.at[group_of(ARRIVE, kind)]
 
-    def leaving(kind):
-        return send_sem.at[group_of(LEAVE, kind)]
-
     @pl.when(corner_sender)
     def _():
         pltpu.make_async_copy(first_rows, first_rows, load_sem.at[1]).wait()
@@ -552,15 +552,10 @@
         adjust(state.at[7], r, 15, 0.5 * a)
 
 
-def write_out(state, faces_new, state_hbm, faces_hbm, sem):
-    copies = [
-        pltpu.make_async_copy(state, state_hbm, sem.at[0]),
-        pltpu.make_async_copy(faces_new, faces_hbm, sem.at[1]),
-    ]
-    for copy in copies:
-        copy.start()
-    for copy in copies:
-        copy.wait()
+def write_out(state, faces_new, state_hbm, faces_hbm, tokens, sem):
+    pltpu.make_async_copy(state, state_hbm, sem).start()
+    pltpu.make_async_copy(faces_new, faces_hbm, sem).start()
+    pltpu.make_async_copy(tokens, tokens, sem).wait()
 
 
 def on_device(cells, faces):
@@ -593,7 +588,7 @@
             pltpu.VMEM((2, 2, 4, 128), f32),
             pltpu.VMEM((704, 1, 128), f32),
             pltpu.SemaphoreType.DMA((2,)),
-            pltpu.SemaphoreType.DMA((len(LEAVE),)),
+            pltpu.SemaphoreType.DMA,
             pltpu.SemaphoreType.DMA((len(ARRIVE),)),
             pltpu.SemaphoreType.REGULAR,
             pltpu.SemaphoreType.REGULAR,
@@ -607,7 +602,7 @@
         out_shape=tuple(jax.ShapeDtypeStruct(shape, f32) for shape in shapes),
         in_specs=[pl.BlockSpec(memory_space=pltpu.VMEM)] * 2,
         out_specs=(pl.BlockSpec(memory_space=pl.ANY),) * 2,
-        scratch_shapes=[pltpu.SemaphoreType.DMA((2,))],
+        scratch_shapes=[pltpu.VMEM((11, 4, 16, 128), f32), pltpu.SemaphoreType.DMA],
         name="write_out",
     )(*(pltpu.with_memory_space_constraint(x, pltpu.VMEM) for x in outputs))
 

time: 29.6 us -> 29.6 us (level)
  no operation moved by 1% of the time
where the time goes in v6:
time: 29.6 us; the launch traced here: 29.2 us
  Pallas kernels  28.5 us (96%)
  between operations  0.64 us (2%)
    pallas_call x1, Pallas kernels, on_device(): pl.pallas_call(kernel, out_shape=tuple((pltpu.VMEM(shape, f32) for shape...  27.8 us
    pallas_call x1, Pallas kernels, on_device(): pl.pallas_call(write_out, out_shape=tuple((jax.ShapeDtypeStruct(shape, f3...  0.74 us

profile of v6, /device:TPU:6, one launch (start us, length us, event | category | flops | bytes accessed | tf_op | source)
XLA Modules:
  0.0 29.2 jit_solution(5672490778110478534)
XLA Ops:
  0.6 27.8 %section.1 = (f32[8,4,16,128]{3,2,1,0:T(8,128)S(1)}, f32[3,4,16,128]{3,2,1,0:T(8,128)S(1)}) custom-call(f32[8,4,16,128]{3,2,1,0:T(8,128)} %cells_hbm.1, f32[3,4,16,128]{3,2,1,0:T(8,128)} %faces_hbm.1), custom_call_target="tpu_custom_call" | custom-call | tf_op jit(solution)/shard_map/section/pallas_call | solution.py:564
  28.4 0.7 %write_out.1 = (f32[8,4,16,128]{3,2,1,0:T(8,128)}, f32[3,4,16,128]{3,2,1,0:T(8,128)}) custom-call(f32[8,4,16,128]{3,2,1,0:T(8,128)S(1)} %get-tuple-element.4.state, f32[3,4,16,128]{3,2,1,0:T(8,128)S(1)} %get-tuple-element.5.faces_new), custom_call_target="tpu_custom_call" | custom-call | tf_op jit(solution)/shard_map/write_out/pallas_call | solution.py:600
